TPU v7x, 8 devices: a whole 2x2x1 slice. The times are simulated.
8 devices in a mesh: dp: 2 (over z, y), tp: 4 (over x, core).
Axes of the slice: x: 2, y: 2, z: 1, core: 2. Of those that a mesh axis runs over, the one named last changes fastest.
Arguments:
- x: bfloat16 [512, 4096], P('dp'), parts along dimension 0
- ln_attn_gamma: float32 [4096], replicated
- ln_attn_beta: float32 [4096], replicated
- ln_mlp_gamma: float32 [4096], replicated
- ln_mlp_beta: float32 [4096], replicated
- w_qkv: bfloat16 [4096, 8, 6, 128], P(None, 'tp')
- w_out: bfloat16 [8, 4, 128, 4096], P('tp')
- w_up: bfloat16 [4096, 16384], P(None, 'tp')
- w_down: bfloat16 [16384, 4096], P('tp')
- k_cache: bfloat16 [512, 8, 256, 128], P('dp', 'tp'), parts along dimension 0
- v_cache: bfloat16 [512, 8, 256, 128], P('dp', 'tp'), parts along dimension 0
- positions: int32 [512], P('dp'), parts along dimension 0
Outputs:
- output 1: bfloat16 [512, 4096], P('dp'), parts along dimension 0
- output 2: bfloat16 [512, 8, 256, 128], P('dp', 'tp'), parts along dimension 0
- output 3: bfloat16 [512, 8, 256, 128], P('dp', 'tp'), parts along dimension 0
There are 2 independent parts. A program takes and returns all parts, laid end to end along the dimension named above; an argument that names none is the same for every part.
All inputs are finite; a program needn't handle non-finite values.
Results may differ from a plain program's by a relative error of at most 0.0101396.
Values are sent between devices in bfloat16 or wider.
A program may use at most 1 GiB of HBM per device.

v0:
```python
import jax
import jax.numpy as jnp
from jax import lax
from jax.sharding import PartitionSpec as P

LN_EPS = 1e-5
ROPE_BASE = 10000.0
NEG_BIG = -1e30


def layer_norm(act_rows, ln_gamma, ln_beta):
    rows_f32 = act_rows.astype(jnp.float32)
    row_mean = jnp.mean(rows_f32, axis=-1, keepdims=True)
    centred = rows_f32 - row_mean
    row_var = jnp.mean(centred * centred, axis=-1, keepdims=True)
    return (centred * lax.rsqrt(row_var + LN_EPS) * ln_gamma + ln_beta).astype(jnp.bfloat16)


def apply_rotary(vectors, cos_t, sin_t):
    half_width = vectors.shape[-1] // 2
    as_f32 = vectors.astype(jnp.float32)
    lower_half = as_f32[..., :half_width]
    upper_half = as_f32[..., half_width:]
    return jnp.concatenate([lower_half * cos_t - upper_half * sin_t, upper_half * cos_t + lower_half * sin_t], axis=-1).astype(jnp.bfloat16)


def attend_local(attn_in, w_qkv, k_cache, v_cache, positions):
    n_query = w_qkv.shape[2] - 2
    head_dim = w_qkv.shape[3]
    qkv_rows = jnp.einsum('bd,dgjh->bgjh', attn_in, w_qkv, preferred_element_type=jnp.float32).astype(jnp.bfloat16)
    inv_freq = ROPE_BASE ** (-2.0 * jnp.arange(head_dim // 2, dtype=jnp.float32) / head_dim)
    angles = positions.astype(jnp.float32)[:, None] * inv_freq[None, :]
    cos_t = jnp.cos(angles)
    sin_t = jnp.sin(angles)
    queries = apply_rotary(qkv_rows[:, :, :n_query], cos_t[:, None, None, :], sin_t[:, None, None, :])
    new_key = apply_rotary(qkv_rows[:, :, n_query], cos_t[:, None, :], sin_t[:, None, :])
    new_value = qkv_rows[:, :, n_query + 1]
    slot_ids = jnp.arange(k_cache.shape[2])
    write_mask = (slot_ids[None, :] == positions[:, None])[:, None, :, None]
    keys_all = jnp.where(write_mask, new_key[:, :, None, :], k_cache)
    values_all = jnp.where(write_mask, new_value[:, :, None, :], v_cache)
    valid_mask = (slot_ids[None, :] <= positions[:, None])[:, None, None, :]
    scores = jnp.einsum('bgqh,bgsh->bgqs', queries, keys_all, preferred_element_type=jnp.float32) * (head_dim ** -0.5)
    scores = jnp.where(valid_mask, scores, NEG_BIG)
    attn_probs = jax.nn.softmax(scores, axis=-1).astype(jnp.bfloat16)
    context = jnp.einsum('bgqs,bgsh->bgqh', attn_probs, values_all, preferred_element_type=jnp.float32).astype(jnp.bfloat16)
    return context, keys_all, values_all


def solution(mesh):
    row_spec = P('dp', None)
    vec_spec = P(None)
    cache_spec = P('dp', 'tp', None, None)

    def device_step(x, ln_attn_gamma, ln_attn_beta, ln_mlp_gamma, ln_mlp_beta, w_qkv, w_out, w_up, w_down, k_cache, v_cache, positions):
        attn_in = layer_norm(x, ln_attn_gamma, ln_attn_beta)
        mlp_in = layer_norm(x, ln_mlp_gamma, ln_mlp_beta)
        context, keys_all, values_all = attend_local(attn_in, w_qkv, k_cache, v_cache, positions)
        attn_part = jnp.einsum('bgqh,gqhd->bd', context, w_out, preferred_element_type=jnp.float32).astype(jnp.bfloat16)
        attn_total = lax.psum(attn_part, 'tp')
        hidden = jax.nn.gelu(jnp.dot(mlp_in, w_up, preferred_element_type=jnp.float32), approximate=False).astype(jnp.bfloat16)
        mlp_part = jnp.dot(hidden, w_down, preferred_element_type=jnp.float32).astype(jnp.bfloat16)
        mlp_total = lax.psum(mlp_part, 'tp')
        layer_out = (x.astype(jnp.float32) + attn_total.astype(jnp.float32) + mlp_total.astype(jnp.float32)).astype(jnp.bfloat16)
        return layer_out, keys_all, values_all

    return jax.shard_map(device_step, mesh=mesh, in_specs=(row_spec, vec_spec, vec_spec, vec_spec, vec_spec, P(None, 'tp', None, None), P('tp', None, None, None), P(None, 'tp'), P('tp', None), cache_spec, cache_spec, P('dp')), out_specs=(row_spec, cache_spec, cache_spec), check_vma=False)
```

profile of v0, /device:TPU:0, one launch (start us, length us, event | category | flops | bytes accessed | tf_op | source)
XLA Modules:
  0.0 268.8 jit_solution(16618701558992750693)
XLA Ops:
  7.2 0.0 all-reduce.3.cloned.1.call-start
  7.2 0.7 convert_element_type.60
  7.9 1.5 iota_compare_fusion.1
  9.4 2.0 convert_reduce_fusion
  11.3 2.3 fusion.10
  13.6 0.0 copy-start
  13.7 31.0 %copy.15 = bf16[4096,2,6,128]{0,3,2,1:T(8,128)(2,1)} copy(bf16[4096,2,6,128]{3,1,2,0:T(2,128)(2,1)} %param.17) | data formatting | bytes 25165824 | tf_op args[5]
  44.7 6.8 %fusion.26 = f32[256,1536]{0,1:S(1)} fusion(bf16[4096,1536]{0,1:T(8,128)(2,1)} %bitcast.27, bf16[256,4096]{1,0:T(8,128)(2,1)S(1)} %copy-done, f32[4096]{0:T(1024)S(1)} %copy-done.4, f32[4096]{0:T(1024)S(1)} %copy-done.5, f32[256]{0:T(256)S(1)} %add_rsqrt_fusion, f32[256]{0:T(256)S(1)} %broadcast_multiply_fusion), kind=kOutput, calls=%fused_computation.40 | convolution fusion | flops 3227516928 | bytes 16287744
  51.5 0.1 convert_element_type.58
  51.6 0.1 slice_convert_fusion
  51.7 0.3 multiply_cosine_fusion
  52.1 0.8 copy.16
  52.9 0.1 copy.18
  53.0 0.1 subtract_convert_fusion
  53.2 0.3 copy.17
  53.5 23.7 %fusion.131 = bf16[256,4096]{1,0:T(8,128)(2,1)S(1)} fusion(bf16[4096,4096]{1,0:T(8,128)(2,1)} %param.19, bf16[256,4096]{1,0:T(8,128)(2,1)S(1)} %copy-done, f32[4096]{0:T(1024)} %param.16, f32[4096]{0:T(1024)} %param.15, f32[256]{0:T(256)S(1)} %add_rsqrt_fusion, f32[256]{0:T(256)S(1)} %broadcast_multiply_fusion), kind=kOutput, calls=%fused_computation.23.clone.clone.1 | convolution fusion | flops 8664383488 | bytes 37783552 | tf_op jit(solution)/shard_map/dot_general | solution.py:61
  77.2 16.8 %convolution_convert_fusion = bf16[256,4096]{1,0:T(8,128)(2,1)} fusion(bf16[4096,4096]{1,0:T(8,128)(2,1)} %param.20, bf16[256,4096]{1,0:T(8,128)(2,1)S(1)} %fusion.131), kind=kOutput, calls=%fused_computation.9 | convolution fusion | flops 8590983168 | bytes 37748736 | tf_op jit(solution)/shard_map/dot_general | solution.py:62
  94.1 43.7 %broadcast_select_fusion.1 = (bf16[256,2,256,128]{3,2,1,0:T(8,128)(2,1)}, bf16[256,2,256,128]{3,2,1,0:T(8,128)(2,1)}) fusion(bf16[256,2,256,128]{3,2,1,0:T(8,128)(2,1)} %param.21, pred[256,256]{1,0:T(8,128)(4,1)S(1)} %copy-done.3, bf16[256,2,128]{2,1,0:T(2,128)(2,1)S(1)} %copy-done.1, bf16[256,2,256,128]{3,2,1,0:T(8,128)(2,1)} %param.22, ...), kind=kLoop, calls=%fused_computation.2 | loop fusion | flops 33554432 | bytes 134545408 | tf_op jit(solution)/shard_map/jit(_where)/select_n | solution.py:40
  137.8 16.3 %fusion.112 = (f32[256,2,4]{2,1,0:T(2,128)S(1)}, f32[256,2,4,256]{3,2,1,0:T(4,128)}) fusion(pred[256,256]{1,0:T(8,128)(4,1)S(1)} %copy-done.2, bf16[256,2,4,128]{3,2,1,0:T(4,128)(2,1)S(1)} %copy.17, bf16[256,2,256,128]{3,2,1,0:T(8,128)(2,1)} %get-tuple-element.11), kind=kOutput, calls=%fused_computation.138 | convolution fusion | flops 136315136 | bytes 36249600 | tf_op jit(solution)/shard_map/sub | solution.py:45
  154.1 13.5 %fusion.74 = bf16[256,2,4,128]{3,2,1,0:T(4,128)(2,1)S(1)} fusion(bf16[256,2,256,128]{3,2,1,0:T(8,128)(2,1)} %get-tuple-element.12, f32[256,2,4,256]{3,2,1,0:T(4,128)} %get-tuple-element.18, f32[256,2,4]{2,1,0:T(2,128)S(1)} %get-tuple-element.17), kind=kOutput, calls=%fused_computation.83 | convolution fusion | flops 135266304 | bytes 36184064 | tf_op jit(solution)/shard_map/bgqs,bgsh->bgqh/dot_general | solution.py:46
  167.6 6.9 %fusion.1 = bf16[256,4096]{1,0:T(8,128)(2,1)} fusion(bf16[2,4,128,4096]{3,2,1,0:T(8,128)(2,1)} %param.18, bf16[256,2,4,128]{3,2,1,0:T(4,128)(2,1)S(1)} %fusion.74), kind=kOutput, calls=%fused_computation.8 | convolution fusion | flops 2148532224 | bytes 11010048 | tf_op jit(solution)/shard_map/bgqh,gqhd->bd/dot_general | solution.py:59
  174.6 0.0 all-reduce.3.cloned.1.call-update
  174.6 82.7 %all-reduce.3.cloned.1.call-done = (bf16[256,4096]{1,0:T(8,128)(2,1)}, bf16[256,4096]{1,0:T(8,128)(2,1)}) async-done(((bf16[256,4096]{1,0:T(8,128)(2,1)}, bf16[256,4096]{1,0:T(8,128)(2,1)}), (bf16[256,4096]{1,0:T(8,128)(2,1)}, bf16[256,4096]{1,0:T(8,128)(2,1)})) %all-reduce.3.cloned.1.call-update) | async-done | bytes 4194320 | tf_op jit(solution)/shard_map/psum | solution.py:63
  257.3 4.6 %fusion.12 = bf16[256,4096]{1,0:T(8,128)(2,1)} fusion(bf16[256,4096]{1,0:T(8,128)(2,1)S(1)} %copy-done, bf16[256,4096]{1,0:T(8,128)(2,1)} %get-tuple-element.3, bf16[256,4096]{1,0:T(8,128)(2,1)} %get-tuple-element.4), kind=kLoop, calls=%fused_computation.20 | loop fusion | flops 6291456 | bytes 8388608 | tf_op jit(solution)/shard_map/convert_element_type | solution.py:64
  (18 shorter events, 0.2 us)
Async XLA Ops:
  7.2 250.2 %all-reduce.3.cloned.1.call-start = ((), (), s32[]{:S(2)}) async-start(), calls=%async_computation | async-start | bytes 8388608 | tf_op jit(solution)/shard_map/psum | solution.py:63
  13.6 31.1 %copy-start = (bf16[256,4096]{1,0:T(8,128)(2,1)S(1)}, bf16[256,4096]{1,0:T(8,128)(2,1)}, u32[]{:S(2)}) copy-start(bf16[256,4096]{1,0:T(8,128)(2,1)} %param.12) | copy-start | bytes 6291460
  13.6 31.1 %copy-start.4 = (f32[4096]{0:T(1024)S(1)}, f32[4096]{0:T(1024)}, u32[]{:S(2)}) copy-start(f32[4096]{0:T(1024)} %param.14) | copy-start | bytes 49156
  13.7 31.1 %copy-start.5 = (f32[4096]{0:T(1024)S(1)}, f32[4096]{0:T(1024)}, u32[]{:S(2)}) copy-start(f32[4096]{0:T(1024)} %param.13) | copy-start | bytes 49156
  77.2 16.9 %copy-start.1 = (bf16[256,2,128]{2,1,0:T(2,128)(2,1)S(1)}, bf16[256,2,128]{2,1,0:T(2,128)(2,1)}, u32[]{:S(2)}) copy-start(bf16[256,2,128]{2,1,0:T(2,128)(2,1)} %copy.16) | copy-start | bytes 393220
  77.2 16.9 %copy-start.3 = (pred[256,256]{1,0:T(8,128)(4,1)S(1)}, pred[256,256]{1,0:T(8,128)(4,1)}, u32[]{:S(2)}) copy-start(pred[256,256]{1,0:T(8,128)(4,1)} %get-tuple-element.16) | copy-start | bytes 196612
  94.1 43.8 %copy-start.2 = (pred[256,256]{1,0:T(8,128)(4,1)S(1)}, pred[256,256]{1,0:T(8,128)(4,1)}, u32[]{:S(2)}) copy-start(pred[256,256]{1,0:T(8,128)(4,1)} %get-tuple-element.15) | copy-start | bytes 196612
Sparse Core Ops, SparseCore 0:
  174.7 82.5 all-reduce.2
where the time goes:
time: 270 us; the launch traced here: 269 us
  matrix products  84 us (31%)
  waiting for transfers between devices  82.7 us (31%)
  other arithmetic  55.5 us (21%)
  local copies, waits for them, and re-layouts  32.3 us (12%)
  between operations  14.2 us (5%)
    psum x1, waiting for transfers between devices, device_step(): mlp_total = lax.psum(mlp_part, 'tp')  82.7 us
    select_n x1, other arithmetic, attend_local(): keys_all = jnp.where(write_mask, new_key[:, :, None, :], k_cache)  43.7 us
    unnamed x13, local copies, waits for them, and re-layouts  31.1 us
    dot_general x1, matrix products, device_step(): jnp.dot(mlp_in, w_up, preferred_element_type=jnp.float32)  23.7 us
    dot_general x1, matrix products, device_step(): jnp.dot(hidden, w_down, preferred_element_type=jnp.float32)  16.8 us
    sub x1, matrix products, attend_local(): attn_probs = jax.nn.softmax(scores, axis=-1).astype(jnp.bfloat16)  16.3 us
    dot_general x1, matrix products, attend_local(): jnp.einsum('bgqs,bgsh->bgqh', attn_probs, values_all, preferred_element_t...  13.5 us
    dot_general x1, matrix products, device_step(): jnp.einsum('bgqh,gqhd->bd', context, w_out, preferred_element_type=jnp.fl...  6.94 us
  transfers between devices with their start and end apart: 1, of which 1 were waited for; matrix products, arithmetic and copies ran while one was open for 0% of the time, Pallas kernels for 0%

commit v1 on v0

v1 whole, which is shorter than its diff:
```python
import jax
import jax.numpy as jnp
from jax import lax
from jax.experimental import pallas as pl
from jax.experimental.pallas import tpu as pltpu
from jax.sharding import PartitionSpec as P

LN_EPS = 1e-5
ROPE_BASE = 10000.0
NEG_BIG = -1e30
BF16 = jnp.bfloat16
F32 = jnp.float32
ANY = pl.BlockSpec(memory_space=pl.ANY)


QKV_CHUNK = 512
QKV_SLOTS = 6
FF_BLOCK = 512
FF_SLOTS = 6
LN_ROWS = 16


def project_kernel(x_hbm, vec_hbm, rot_hbm, wq_hbm, wu_hbm, wd_hbm,
                   q_hbm, kv_hbm, m_hbm,
                   x_s, vec_s, rot_s, attn_s, mlp_s, hid_s, wq_s, wqf_s, acc_s, ring_s, q_s, kv_s, m_s,
                   in_sem, wq_sem, ring_sem, out_sem):
    rows, width = x_s.shape
    n_chunk = width // QKV_CHUNK
    lines = wq_hbm.shape[0] // width
    n_up = wu_hbm.shape[1] // FF_BLOCK
    n_down = wd_hbm.shape[1] // FF_BLOCK
    n_ff = n_up + n_down

    copies = [
        pltpu.make_async_copy(x_hbm, x_s, in_sem.at[0]),
        pltpu.make_async_copy(vec_hbm, vec_s, in_sem.at[1]),
        pltpu.make_async_copy(rot_hbm, rot_s, in_sem.at[2]),
    ]
    for c in copies:
        c.start()

    def wq_copy(c, slot):
        return pltpu.make_async_copy(wq_hbm.at[pl.ds(c * QKV_CHUNK * lines, QKV_CHUNK * lines), :], wq_s.at[slot], wq_sem.at[slot])

    quarter = width // 4

    def ff_start(w_hbm, b, slot):
        for p in range(4):
            pltpu.make_async_copy(w_hbm.at[pl.ds(p * quarter, quarter), pl.ds(b * FF_BLOCK, FF_BLOCK)],
                                  ring_s.at[slot, pl.ds(p * quarter, quarter), :], ring_sem.at[slot]).start()

    def ff_wait(slot):
        pltpu.make_async_copy(wu_hbm.at[:, pl.ds(0, FF_BLOCK)], ring_s.at[slot], ring_sem.at[slot]).wait()

    for c in range(QKV_SLOTS):
        wq_copy(c, c).start()
    for b in range(FF_SLOTS):
        ff_start(wu_hbm, b, b)

    for c in copies:
        c.wait()

    def ln_body(i, carry):
        r = pl.ds(pl.multiple_of(i * LN_ROWS, LN_ROWS), LN_ROWS)
        xf = x_s[r, :].astype(F32)
        mean = jnp.mean(xf, axis=-1, keepdims=True)
        cen = xf - mean
        var = jnp.mean(cen * cen, axis=-1, keepdims=True)
        nrm = cen * lax.rsqrt(var + LN_EPS)
        attn_s[r, :] = (nrm * vec_s[0:1, :] + vec_s[1:2, :]).astype(BF16)
        mlp_s[r, :] = (nrm * vec_s[2:3, :] + vec_s[3:4, :]).astype(BF16)
        return carry

    lax.fori_loop(0, rows // LN_ROWS, ln_body, 0)

    for c in range(n_chunk):
        slot = c % QKV_SLOTS
        wq_copy(c, slot).wait()
        wqf_s[...] = wq_s[slot].astype(F32)
        if c + QKV_SLOTS < n_chunk:
            wq_copy(c + QKV_SLOTS, slot).start()
        lhs = attn_s[:, c * QKV_CHUNK:(c + 1) * QKV_CHUNK]
        for pair in range(lines // 2):
            w = jnp.concatenate([wqf_s[pl.ds(2 * pair + e, QKV_CHUNK, stride=lines), :].astype(BF16) for e in range(2)], axis=1)
            part = jnp.dot(lhs, w, preferred_element_type=F32)
            if c == 0:
                acc_s[:, pair * 256:(pair + 1) * 256] = part
            else:
                acc_s[:, pair * 256:(pair + 1) * 256] += part

    cos_f = rot_s[:, 0:128]
    sin_f = rot_s[:, 128:256]
    n_slot = lines // 2
    n_q = n_slot - 2
    for j in range(n_slot):
        for g in range(2):
            col = (2 * j + g) * 128
            u = acc_s[:, col:col + 128].astype(BF16).astype(F32)
            if j < n_q + 1:
                u = (u * cos_f + pltpu.roll(u, 64, 1) * sin_f).astype(BF16).astype(F32)
            if j < n_q:
                q_s[pl.ds((g * n_q + j) * rows, rows), :] = u
            else:
                kv_s[pl.ds(((j - n_q) * 2 + g) * rows, rows), :] = u
    q_out = pltpu.make_async_copy(q_s, q_hbm, out_sem.at[0])
    kv_out = pltpu.make_async_copy(kv_s, kv_hbm, out_sem.at[1])
    q_out.start()
    kv_out.start()

    def up_body(b, carry):
        slot = lax.rem(b, FF_SLOTS)
        ff_wait(slot)
        pre = jnp.dot(mlp_s[...], ring_s[slot], preferred_element_type=F32)
        act = 0.5 * pre * (1.0 + lax.erf(pre * (0.5 ** 0.5)))
        hid_s[:, pl.ds(pl.multiple_of(b * FF_BLOCK, FF_BLOCK), FF_BLOCK)] = act.astype(BF16)
        nxt = b + FF_SLOTS

        @pl.when(nxt < n_up)
        def _():
            ff_start(wu_hbm, nxt, slot)

        @pl.when(nxt >= n_up)
        def _():
            ff_start(wd_hbm, nxt - n_up, slot)
        return carry

    lax.fori_loop(0, n_up, up_body, 0)

    def m_copy(b):
        cols = pl.ds(pl.multiple_of(b * FF_BLOCK, FF_BLOCK), FF_BLOCK)
        return pltpu.make_async_copy(m_s.at[:, cols], m_hbm.at[:, cols], out_sem.at[2])

    def down_body(b, carry):
        slot = lax.rem(b + n_up, FF_SLOTS)
        ff_wait(slot)
        m_s[:, pl.ds(pl.multiple_of(b * FF_BLOCK, FF_BLOCK), FF_BLOCK)] = jnp.dot(hid_s[...], ring_s[slot], preferred_element_type=F32)
        m_copy(b).start()
        nxt = b + FF_SLOTS

        @pl.when(nxt < n_down)
        def _():
            ff_start(wd_hbm, nxt, slot)
        return carry

    lax.fori_loop(0, n_down, down_body, 0)
    pltpu.make_async_copy(m_s, m_hbm, out_sem.at[2]).wait()
    q_out.wait()
    kv_out.wait()


def project(x, vecs, rot, wq, wu, wd):
    rows, width = x.shape
    hid = wu.shape[1]
    lines = wq.shape[0] // width
    n_head = (lines // 2 - 2) * 2
    return pl.pallas_call(
        project_kernel,
        name='project',
        in_specs=[ANY] * 6,
        out_specs=[ANY] * 3,
        out_shape=[
            jax.ShapeDtypeStruct((n_head * rows, 128), F32),
            jax.ShapeDtypeStruct((4 * rows, 128), F32),
            jax.ShapeDtypeStruct((rows, width), F32),
        ],
        scratch_shapes=[
            pltpu.VMEM((rows, width), BF16),
            pltpu.VMEM(vecs.shape, F32),
            pltpu.VMEM(rot.shape, F32),
            pltpu.VMEM((rows, width), BF16),
            pltpu.VMEM((rows, width), BF16),
            pltpu.VMEM((rows, hid), BF16),
            pltpu.VMEM((QKV_SLOTS, QKV_CHUNK * lines, 128), BF16),
            pltpu.VMEM((QKV_CHUNK * lines, 128), F32),
            pltpu.VMEM((rows, lines * 128), F32),
            pltpu.VMEM((FF_SLOTS, width, FF_BLOCK), BF16),
            pltpu.VMEM((n_head * rows, 128), F32),
            pltpu.VMEM((4 * rows, 128), F32),
            pltpu.VMEM((rows, width), F32),
            pltpu.SemaphoreType.DMA((3,)),
            pltpu.SemaphoreType.DMA((QKV_SLOTS,)),
            pltpu.SemaphoreType.DMA((FF_SLOTS,)),
            pltpu.SemaphoreType.DMA((3,)),
        ],
        compiler_params=pltpu.CompilerParams(vmem_limit_bytes=63 * 1024 * 1024),
        cost_estimate=pl.CostEstimate(flops=22 * 10 ** 9, bytes_accessed=90 * 10 ** 6, transcendentals=0),
    )(x, vecs, rot, wq, wu, wd)


ROW_BLOCK = 8
KV_SLOTS = 8
KV_AHEAD = 4
OUT_BLOCK = 512


def attend_kernel(row0, n_rows, pos_ref, core_ref, q_hbm, kv_hbm, m_hbm, wo_hbm, kc_hbm, vc_hbm, *rest):
    n_alias = 2 if row0 else 0
    ko_hbm, vo_hbm, send_hbm, keep_hbm = rest[n_alias:n_alias + 4]
    q_s, kv_s, m_s, wo_s, kbuf, vbuf, ctx_s, send_s, keep_s, kin_sem, vin_sem, kout_sem, vout_sem, sem = rest[n_alias + 4:]
    n_blk = n_rows // ROW_BLOCK
    total_rows = q_hbm.shape[0] // 8

    def block(ref, i):
        return ref.at[pl.ds(row0 + i * ROW_BLOCK, ROW_BLOCK)]

    def start_in(i, slot):
        pltpu.make_async_copy(block(kc_hbm, i), kbuf.at[slot], kin_sem.at[slot]).start()
        pltpu.make_async_copy(block(vc_hbm, i), vbuf.at[slot], vin_sem.at[slot]).start()

    def wait_in(slot):
        pltpu.make_async_copy(block(kc_hbm, 0), kbuf.at[slot], kin_sem.at[slot]).wait()
        pltpu.make_async_copy(block(vc_hbm, 0), vbuf.at[slot], vin_sem.at[slot]).wait()

    def start_out(i, slot):
        pltpu.make_async_copy(kbuf.at[slot], block(ko_hbm, i), kout_sem.at[slot]).start()
        pltpu.make_async_copy(vbuf.at[slot], block(vo_hbm, i), vout_sem.at[slot]).start()

    def wait_out(slot):
        pltpu.make_async_copy(kbuf.at[slot], block(ko_hbm, 0), kout_sem.at[slot]).wait()
        pltpu.make_async_copy(vbuf.at[slot], block(vo_hbm, 0), vout_sem.at[slot]).wait()

    q_in = pltpu.make_async_copy(q_hbm, q_s, sem.at[0])
    kv_in = pltpu.make_async_copy(kv_hbm, kv_s, sem.at[1])
    q_in.start()
    kv_in.start()
    for i in range(min(KV_AHEAD, n_blk)):
        start_in(i, i)
    wo_in = pltpu.make_async_copy(wo_hbm, wo_s, sem.at[2])
    m_in = pltpu.make_async_copy(m_hbm.at[pl.ds(row0, n_rows), :], m_s, sem.at[3])
    wo_in.start()
    m_in.start()
    q_in.wait()
    kv_in.wait()

    slot_ids = lax.broadcasted_iota(jnp.int32, (8, 256), 1)
    tile_ids = lax.broadcasted_iota(jnp.int32, (16, 128), 0)
    first = lax.broadcasted_iota(jnp.int32, (8, 128), 0) < 4
    scale = 128 ** -0.5

    def body(i, carry):
        slot = lax.rem(i, KV_SLOTS)
        nxt = i + KV_AHEAD

        @pl.when(nxt < n_blk)
        def _():
            nslot = lax.rem(nxt, KV_SLOTS)

            @pl.when(nxt >= KV_SLOTS)
            def _():
                wait_out(nslot)
            start_in(nxt, nslot)

        wait_in(slot)
        pos = [pos_ref[row0 + i * ROW_BLOCK + r] for r in range(ROW_BLOCK)]
        for r in range(ROW_BLOCK):
            base = pl.multiple_of((pos[r] // 16) * 16, 16)
            hit = tile_ids == pos[r] - base
            b = row0 + i * ROW_BLOCK + r
            for g in range(2):
                for buf, which in ((kbuf, 0), (vbuf, 1)):
                    new = kv_s[pl.ds((which * 2 + g) * total_rows + b, 1), :]
                    old = buf[slot, r, g, pl.ds(base, 16), :].astype(F32)
                    buf[slot, r, g, pl.ds(base, 16), :] = jnp.where(hit, new, old).astype(BF16)
        scores = []
        for r in range(ROW_BLOCK):
            b = row0 + i * ROW_BLOCK + r
            q = q_s[pl.ds(b, 8, stride=total_rows), :]
            zero = jnp.zeros_like(q)
            q2 = jnp.concatenate([jnp.where(first, q, zero), jnp.where(first, zero, q)], axis=1).astype(BF16)
            k2 = jnp.concatenate([kbuf[slot, r, 0], kbuf[slot, r, 1]], axis=1)
            s = lax.dot_general(q2, k2, (((1,), (1,)), ((), ())), preferred_element_type=F32) * scale
            scores.append(jnp.where(slot_ids <= pos[r], s, NEG_BIG))
        s = jnp.concatenate(scores, axis=0)
        e = jnp.exp(s - jnp.max(s, axis=-1, keepdims=True))
        p = (e / jnp.sum(e, axis=-1, keepdims=True)).astype(BF16)
        for r in range(ROW_BLOCK):
            v2 = jnp.concatenate([vbuf[slot, r, 0], vbuf[slot, r, 1]], axis=1)
            c = jnp.dot(p[8 * r:8 * r + 8], v2, preferred_element_type=F32)
            ctx_s[pl.ds(i * ROW_BLOCK + r, 8, stride=n_rows), :] = jnp.where(first, c[:, :128], c[:, 128:])
        start_out(i, slot)
        return carry

    lax.fori_loop(0, n_blk, body, 0)

    ctx = jnp.concatenate([ctx_s[pl.ds(h * n_rows, n_rows), :] for h in range(8)], axis=1).astype(BF16)
    wo_in.wait()
    m_in.wait()
    core = core_ref[0]
    half = m_s.shape[1] // 2

    def out_body(n, carry):
        dst = pl.ds(pl.multiple_of(n * OUT_BLOCK, OUT_BLOCK), OUT_BLOCK)
        for mine, stage, hbm in ((False, send_s, send_hbm), (True, keep_s, keep_hbm)):
            side = core if mine else 1 - core
            src = pl.ds(pl.multiple_of(side * half + n * OUT_BLOCK, OUT_BLOCK), OUT_BLOCK)
            part = jnp.dot(ctx, wo_s[:, src], preferred_element_type=F32) + m_s[:, src]
            stage[:, dst] = part.astype(stage.dtype)
            pltpu.make_async_copy(stage.at[:, dst], hbm.at[:, dst], sem.at[4 + mine]).start()
        return carry

    lax.fori_loop(0, half // OUT_BLOCK, out_body, 0)
    pltpu.make_async_copy(send_s, send_hbm, sem.at[4]).wait()
    pltpu.make_async_copy(keep_s, keep_hbm, sem.at[5]).wait()
    for i in range(max(0, n_blk - KV_SLOTS), n_blk):
        wait_out(i % KV_SLOTS)


def attend(row0, n_rows, pos, core, q, kv, m, wo, kc, vc, prev):
    import functools
    rows, width = m.shape
    n_in = 8
    alias = {} if prev is None else {n_in: 0, n_in + 1: 1}
    extra = () if prev is None else tuple(prev)
    smem = pl.BlockSpec(memory_space=pltpu.SMEM)
    return pl.pallas_call(
        functools.partial(attend_kernel, row0, n_rows),
        name='attend',
        in_specs=[smem, smem] + [ANY] * (6 + len(extra)),
        out_specs=[ANY] * 4,
        out_shape=[
            jax.ShapeDtypeStruct(kc.shape, BF16),
            jax.ShapeDtypeStruct(vc.shape, BF16),
            jax.ShapeDtypeStruct((n_rows, width // 2), BF16),
            jax.ShapeDtypeStruct((n_rows, width // 2), F32),
        ],
        input_output_aliases=alias,
        scratch_shapes=[
            pltpu.VMEM(q.shape, F32),
            pltpu.VMEM(kv.shape, F32),
            pltpu.VMEM((n_rows, width), F32),
            pltpu.VMEM(wo.shape, BF16),
            pltpu.VMEM((KV_SLOTS, ROW_BLOCK) + kc.shape[1:], BF16),
            pltpu.VMEM((KV_SLOTS, ROW_BLOCK) + vc.shape[1:], BF16),
            pltpu.VMEM((8 * n_rows, 128), F32),
            pltpu.VMEM((n_rows, width // 2), BF16),
            pltpu.VMEM((n_rows, width // 2), F32),
            pltpu.SemaphoreType.DMA((KV_SLOTS,)),
            pltpu.SemaphoreType.DMA((KV_SLOTS,)),
            pltpu.SemaphoreType.DMA((KV_SLOTS,)),
            pltpu.SemaphoreType.DMA((KV_SLOTS,)),
            pltpu.SemaphoreType.DMA((6,)),
        ],
        compiler_params=pltpu.CompilerParams(vmem_limit_bytes=63 * 1024 * 1024),
        cost_estimate=pl.CostEstimate(flops=10 ** 10 * n_rows // 256, bytes_accessed=140 * 10 ** 6 * n_rows // 256, transcendentals=0),
    )(pos, core, q, kv, m, wo, kc, vc, *extra)


CORE_SWAP = [(0, 1), (1, 0), (2, 3), (3, 2)]
CHIP_SWAP = [(0, 2), (2, 0), (1, 3), (3, 1)]
CHUNKS = (256,)


def solution(mesh):
    row_spec = P('dp', None)
    vec_spec = P(None)
    cache_spec = P('dp', 'tp', None, None)

    def device_step(x, ln_attn_gamma, ln_attn_beta, ln_mlp_gamma, ln_mlp_beta, w_qkv, w_out, w_up, w_down, k_cache, v_cache, positions):
        rows, width = x.shape
        core = lax.rem(lax.axis_index('tp'), 2)
        core_arr = core.astype(jnp.int32).reshape(1)
        vecs = jnp.stack([ln_attn_gamma, ln_attn_beta, ln_mlp_gamma, ln_mlp_beta])
        inv_freq = ROPE_BASE ** (-2.0 * jnp.arange(64, dtype=F32) / 128)
        angles = positions.astype(F32)[:, None] * inv_freq[None, :]
        cos_t, sin_t = jnp.cos(angles), jnp.sin(angles)
        rot = jnp.concatenate([cos_t, cos_t, -sin_t, sin_t], axis=1)
        wq = jnp.transpose(w_qkv, (0, 2, 1, 3)).reshape(-1, 128)
        wo = w_out.reshape(-1, width)
        q, kv, m = project(x, vecs, rot, wq, w_up, w_down)
        caches = None
        row0 = 0
        outs = []
        half = width // 2
        for n_rows in CHUNKS:
            ko, vo, send, keep = attend(row0, n_rows, positions, core_arr, q, kv, m, wo, k_cache, v_cache, caches)
            caches = (ko, vo)
            got = lax.ppermute(send, 'tp', CORE_SWAP)
            chip_sum = (keep + got.astype(F32)).astype(BF16)
            other = lax.ppermute(chip_sum, 'tp', CHIP_SWAP)
            x_half = lax.dynamic_slice(x[row0:row0 + n_rows], (0, core * half), (n_rows, half))
            mine = (x_half.astype(F32) + (chip_sum.astype(F32) + other.astype(F32))).astype(BF16)
            partner = lax.ppermute(mine, 'tp', CORE_SWAP)
            is0 = core == 0
            outs.append(jnp.concatenate([jnp.where(is0, mine, partner), jnp.where(is0, partner, mine)], axis=1))
            row0 += n_rows
        out = outs[0] if len(outs) == 1 else jnp.concatenate(outs, axis=0)
        return out, caches[0], caches[1]

    return jax.shard_map(device_step, mesh=mesh, in_specs=(row_spec, vec_spec, vec_spec, vec_spec, vec_spec, P(None, 'tp', None, None), P('tp', None, None, None), P(None, 'tp'), P('tp', None), cache_spec, cache_spec, P('dp')), out_specs=(row_spec, cache_spec, cache_spec), check_vma=False)
```

time: 270 us -> 137 us (0.51)
  Pallas kernels: 0 us -> 94.6 us
  matrix products: 84 us -> 0 us
  waiting for transfers between devices: 82.7 us -> 28.4 us
  other arithmetic: 55.5 us -> 9.37 us
  local copies, waits for them, and re-layouts: 32.3 us -> 0.01 us
  between operations: 14.2 us -> 0.71 us
  starting transfers between devices: 0.04 us -> 3.79 us
    pallas_call x0 -> x2, Pallas kernels: none -> 94.6 us  [the longest x1 52.2 us: attend(): pl.pallas_call(functools.partial(attend_kernel, row0, n_rows), name='atte...]
    psum x1 -> x0, waiting for transfers between devices: 82.7 us -> none  [device_step(): mlp_total = lax.psum(mlp_part, 'tp')]
    dot_general x4 -> x0, matrix products: 61 us -> none  [the longest x1 23.7 us: device_step(): jnp.dot(mlp_in, w_up, preferred_element_type=jnp.float32)]
    select_n x1, other arithmetic: 43.7 us -> 0.14 us  [device_step(): jnp.where(is0, mine, partner)]
    unnamed x13 -> x4, local copies, waits for them, and re-layouts: 31.1 us -> 0.01 us
    ppermute x0 -> x3, waiting for transfers between devices: none -> 28.4 us  [the longest x1 23.5 us: device_step(): other = lax.ppermute(chip_sum, 'tp', CHIP_SWAP)]
    sub x1 -> x0, matrix products: 16.3 us -> none  [attend_local(): attn_probs = jax.nn.softmax(scores, axis=-1).astype(jnp.bfloat16)]
    unnamed x1 -> x0, matrix products: 6.77 us -> none
  transfers between devices with their start and end apart: 1 -> 3, of which waited for: 1 -> 3; matrix products, arithmetic and copies ran while one was open for 0% -> 0% of each run, Pallas kernels for 0% -> 0%
where the time goes in v1:
time: 137 us
  Pallas kernels  94.6 us (69%)
  waiting for transfers between devices  28.4 us (21%)
  other arithmetic  9.37 us (7%)
  starting transfers between devices  3.79 us (3%)
    pallas_call x1, Pallas kernels, attend(): pl.pallas_call(functools.partial(attend_kernel, row0, n_rows), name='atte...  52.2 us
    pallas_call x1, Pallas kernels, project(): pl.pallas_call(project_kernel, name='project', in_specs=[ANY] * 6, out_sp...  42.4 us
    ppermute x1, waiting for transfers between devices, device_step(): other = lax.ppermute(chip_sum, 'tp', CHIP_SWAP)  23.5 us
    ppermute x1, starting transfers between devices, device_step(): other = lax.ppermute(chip_sum, 'tp', CHIP_SWAP)  2.88 us
  transfers between devices with their start and end apart: 3, of which 3 were waited for; matrix products, arithmetic and copies ran while one was open for 0% of the time, Pallas kernels for 0%

profile of v1, /device:TPU:0, one launch (start us, length us, event | category | flops | bytes accessed | tf_op | source)
XLA Modules:
  0.0 136.9 jit_solution(16122495569088188617)
XLA Ops:
  0.7 0.7 convert_element_type.22
  1.3 0.5 multiply_cosine_fusion
  1.9 0.9 pad_maximum_fusion.1.rot_hbm
  2.8 1.5 %pad_maximum_fusion.2.vec_hbm = f32[4,4096]{1,0:T(4,128)} fusion(f32[1,4096]{1,0:T(1,128)} %bitcast.11, f32[1,4096]{1,0:T(1,128)} %bitcast.12, f32[1,4096]{1,0:T(1,128)} %bitcast.13, f32[1,4096]{1,0:T(1,128)} %bitcast.14), kind=kLoop, calls=%fused_computation.8 | loop fusion | flops 49152 | bytes 131072 | tf_op jit(solution)/shard_map/stack | solution.py:362
  4.2 42.4 %project.1 = (f32[2048,128]{1,0:T(8,128)}, f32[1024,128]{1,0:T(8,128)}, f32[256,4096]{1,0:T(8,128)}) custom-call(bf16[256,4096]{1,0:T(8,128)(2,1)} %x_hbm.1, f32[4,4096]{1,0:T(4,128)} %pad_maximum_fusion.2.vec_hbm, f32[256,256]{1,0:T(8,128)} %pad_maximum_fusion.1.rot_hbm, bf16[49152,128]{1,0:T(8,128)(2,1)} %bitcast.9, bf16[4096,4096]{1,0:T(8,128)(2,1)} %wu_hbm.1, ...), custom_call_target="tpu_custom_call" | custom-call | flops 22000001024 | bytes 90000000 | tf_op jit(solution)/shard_map/project/pallas_call | solution.py:156
  46.6 52.2 %attend.1 = (bf16[256,2,256,128]{3,2,1,0:T(8,128)(2,1)}, bf16[256,2,256,128]{3,2,1,0:T(8,128)(2,1)}, bf16[256,2048]{1,0:T(8,128)(2,1)}, f32[256,2048]{1,0:T(8,128)}) custom-call(s32[256]{0:T(256)} %pos_ref.1, s32[1]{0:T(128)} %bitcast.core_ref, f32[2048,128]{1,0:T(8,128)} %get-tuple-element.10.q_hbm, f32[1024,128]{1,0:T(8,128)} %get-tuple-element.11.kv_hbm, ...), custom_call_target="tpu_custom_call" | custom-call | flops 10000000000 | bytes 140000000 | tf_op jit(solution)/shard_map/attend/pallas_call | solution.py:315
  98.8 0.9 collective-permute-start
  99.7 2.3 %collective-permute-done = bf16[256,2048]{1,0:T(8,128)(2,1)S(1)} collective-permute-done((bf16[256,2048]{1,0:T(8,128)(2,1)}, bf16[256,2048]{1,0:T(8,128)(2,1)S(1)}, u32[]{:S(2)}, u32[]{:S(2)}) %collective-permute-start) | collective-permute-done | bytes 1048608 | tf_op jit(solution)/shard_map/ppermute | solution.py:377
  102.0 0.0 copy-start
  102.0 2.1 %add_convert_fusion.1 = bf16[256,2048]{1,0:T(8,128)(2,1)S(1)} fusion(f32[256,2048]{1,0:T(8,128)} %get-tuple-element.13, bf16[256,2048]{1,0:T(8,128)(2,1)S(1)} %collective-permute-done), kind=kLoop, calls=%fused_computation.2 | loop fusion | flops 1572864 | bytes 4194304 | tf_op jit(solution)/shard_map/convert_element_type | solution.py:378
  104.1 0.0 copy-start.1
  104.1 2.9 %collective-permute-start.1 = (bf16[256,2048]{1,0:T(8,128)(2,1)S(1)}, bf16[256,2048]{1,0:T(8,128)(2,1)}, u32[]{:S(2)}, u32[]{:S(2)}) collective-permute-start(bf16[256,2048]{1,0:T(8,128)(2,1)S(1)} %add_convert_fusion.1), channel_id=1, source_target_pairs={{0,2},{2,0},{1,3},{3,1},{4,6},{6,4},{5,7},{7,5}} | collective-permute-start | bytes 3145736 | tf_op jit(solution)/shard_map/ppermute | solution.py:379
  107.0 0.0 copy-done.1
  107.0 23.5 %collective-permute-done.1 = bf16[256,2048]{1,0:T(8,128)(2,1)} collective-permute-done((bf16[256,2048]{1,0:T(8,128)(2,1)S(1)}, bf16[256,2048]{1,0:T(8,128)(2,1)}, u32[]{:S(2)}, u32[]{:S(2)}) %collective-permute-start.1) | collective-permute-done | bytes 1048608 | tf_op jit(solution)/shard_map/ppermute | solution.py:379
  130.4 0.0 copy-done
  130.4 2.1 %add_convert_fusion = bf16[256,2048]{1,0:T(8,128)(2,1)S(1)} fusion(bf16[256,2048]{1,0:T(8,128)(2,1)} %collective-permute-done.1, bf16[256,2048]{1,0:T(8,128)(2,1)} %copy-done.1, bf16[256,4096]{1,0:T(8,128)(2,1)S(1)} %copy-done, s32[]{:T(128)S(6)} %select_n.16), kind=kLoop, calls=%fused_computation.1 | loop fusion | flops 3145728 | bytes 4194308 | tf_op jit(solution)/shard_map/convert_element_type | solution.py:381
  132.5 0.0 collective-permute-start.2
  132.5 2.6 %collective-permute-done.2 = bf16[256,2048]{1,0:T(8,128)(2,1)S(1)} collective-permute-done((bf16[256,2048]{1,0:T(8,128)(2,1)S(1)}, bf16[256,2048]{1,0:T(8,128)(2,1)S(1)}, u32[]{:S(2)}, u32[]{:S(2)}) %collective-permute-start.2) | collective-permute-done | bytes 1048608 | tf_op jit(solution)/shard_map/ppermute | solution.py:382
  135.2 0.1 broadcast_select_fusion.1
  135.3 1.5 %pad_maximum_fusion = bf16[256,4096]{1,0:T(8,128)(2,1)} fusion(bf16[256,2048]{1,0:T(8,128)(2,1)S(1)} %get-tuple-element.18, bf16[256,2048]{1,0:T(8,128)(2,1)S(1)} %get-tuple-element.17), kind=kLoop, calls=%fused_computation | loop fusion | flops 4194304 | bytes 4194304 | tf_op jit(solution)/shard_map/concatenate | solution.py:384
  (1 shorter events, 0.0 us)
Async XLA Ops:
  98.8 3.2 %collective-permute-start = (bf16[256,2048]{1,0:T(8,128)(2,1)}, bf16[256,2048]{1,0:T(8,128)(2,1)S(1)}, u32[]{:S(2)}, u32[]{:S(2)}) collective-permute-start(bf16[256,2048]{1,0:T(8,128)(2,1)} %get-tuple-element.14), channel_id=1, source_target_pairs={{0,1},{1,0},{2,3},{3,2},{4,5},{5,4},{6,7},{7,6}} | collective-permute-start | bytes 3145736 | tf_op jit(solution)/shard_map/ppermute | solution.py:377
  102.0 28.4 %copy-start = (bf16[256,4096]{1,0:T(8,128)(2,1)S(1)}, bf16[256,4096]{1,0:T(8,128)(2,1)}, u32[]{:S(2)}) copy-start(bf16[256,4096]{1,0:T(8,128)(2,1)} %x_hbm.1) | copy-start | bytes 6291460
  104.1 2.9 %copy-start.1 = (bf16[256,2048]{1,0:T(8,128)(2,1)}, bf16[256,2048]{1,0:T(8,128)(2,1)S(1)}, u32[]{:S(2)}) copy-start(bf16[256,2048]{1,0:T(8,128)(2,1)S(1)} %add_convert_fusion.1) | copy-start | bytes 3145732
  104.1 26.3 %collective-permute-start.1 = (bf16[256,2048]{1,0:T(8,128)(2,1)S(1)}, bf16[256,2048]{1,0:T(8,128)(2,1)}, u32[]{:S(2)}, u32[]{:S(2)}) collective-permute-start(bf16[256,2048]{1,0:T(8,128)(2,1)S(1)} %add_convert_fusion.1), channel_id=1, source_target_pairs={{0,2},{2,0},{1,3},{3,1},{4,6},{6,4},{5,7},{7,5}} | collective-permute-start | bytes 3145736 | tf_op jit(solution)/shard_map/ppermute | solution.py:379
  132.5 2.7 %collective-permute-start.2 = (bf16[256,2048]{1,0:T(8,128)(2,1)S(1)}, bf16[256,2048]{1,0:T(8,128)(2,1)S(1)}, u32[]{:S(2)}, u32[]{:S(2)}) collective-permute-start(bf16[256,2048]{1,0:T(8,128)(2,1)S(1)} %add_convert_fusion), channel_id=1, source_target_pairs={{0,1},{1,0},{2,3},{3,2},{4,5},{5,4},{6,7},{7,6}} | collective-permute-start | bytes 3145736 | tf_op jit(solution)/shard_map/ppermute | solution.py:382

commit v2 on v0

v2 whole, which is shorter than its diff:
```python
import jax
import jax.numpy as jnp
import numpy as np
from jax import lax
from jax.experimental import pallas as pl
from jax.experimental.pallas import tpu as pltpu
from jax.sharding import PartitionSpec as P

LN_EPS = 1e-5
ROPE_BASE = 10000.0
NEG_BIG = -1e30
BF16 = jnp.bfloat16
F32 = jnp.float32
ANY = pl.BlockSpec(memory_space=pl.ANY)
SMEM = pl.BlockSpec(memory_space=pltpu.SMEM)
MIB = 1024 * 1024

QKV_CHUNK = 512
LN_ROWS = 16
ROW_BLOCK = 8
SUB_BLOCKS = 2
KV_SLOTS = 12
KV_AHEAD = 8
UP_SLOTS = 3


def front_kernel(pos_ref, x_hbm, ga_hbm, ba_hbm, gm_hbm, bm_hbm, freq_hbm, wq_hbm, wu_hbm, kc_hbm, vc_hbm,
                 ko_hbm, vo_hbm, hid_hbm, ctx_hbm,
                 x_s, vec_s, freq_s, cos_s, sin_s, attn_s, mlp_s, wq_s, wqf_s, acc_s, q_s, kv_s, up_s, hid_s, ctx_s, kbuf, vbuf,
                 in_sem, wq_sem, up_sem, kin_sem, vin_sem, kout_sem, vout_sem, out_sem):
    rows, width = x_s.shape
    n_chunk = width // QKV_CHUNK
    lines = wq_hbm.shape[0] // width
    up_cols = up_s.shape[2]
    n_up = wu_hbm.shape[1] // up_cols
    n_blk = rows // ROW_BLOCK

    small = [pltpu.make_async_copy(x_hbm, x_s, in_sem.at[0])]
    for i, v in enumerate((ga_hbm, ba_hbm, gm_hbm, bm_hbm)):
        small.append(pltpu.make_async_copy(v, vec_s.at[pl.ds(i, 1), :], in_sem.at[1 + i]))
    freq_in = pltpu.make_async_copy(freq_hbm, freq_s, in_sem.at[5])
    freq_in.start()
    for c in small:
        c.start()

    def wq_copy(c):
        return pltpu.make_async_copy(wq_hbm.at[pl.ds(c * QKV_CHUNK * lines, QKV_CHUNK * lines), :], wq_s.at[c], wq_sem.at[c])

    def up_copy(b, slot):
        return pltpu.make_async_copy(wu_hbm.at[:, pl.ds(pl.multiple_of(b * up_cols, up_cols), up_cols)], up_s.at[slot], up_sem.at[slot])

    def block(ref, i):
        return ref.at[pl.ds(i * ROW_BLOCK, ROW_BLOCK)]

    def start_in(i, slot):
        pltpu.make_async_copy(block(kc_hbm, i), kbuf.at[slot], kin_sem.at[slot]).start()
        pltpu.make_async_copy(block(vc_hbm, i), vbuf.at[slot], vin_sem.at[slot]).start()

    def wait_in(slot):
        pltpu.make_async_copy(block(kc_hbm, 0), kbuf.at[slot], kin_sem.at[slot]).wait()
        pltpu.make_async_copy(block(vc_hbm, 0), vbuf.at[slot], vin_sem.at[slot]).wait()

    def start_out(i, slot):
        pltpu.make_async_copy(kbuf.at[slot], block(ko_hbm, i), kout_sem.at[slot]).start()
        pltpu.make_async_copy(vbuf.at[slot], block(vo_hbm, i), vout_sem.at[slot]).start()

    def wait_out(slot):
        pltpu.make_async_copy(kbuf.at[slot], block(ko_hbm, 0), kout_sem.at[slot]).wait()
        pltpu.make_async_copy(vbuf.at[slot], block(vo_hbm, 0), vout_sem.at[slot]).wait()

    for c in range(n_chunk):
        wq_copy(c).start()
    for b in range(UP_SLOTS):
        up_copy(b, b).start()
    for i in range(KV_AHEAD):
        start_in(i, i)

    freq_in.wait()

    def angle_body(b, carry):
        cos_s[pl.ds(b, 1), :] = pos_ref[b].astype(F32) * freq_s[0:1, :]
        return carry

    lax.fori_loop(0, rows, angle_body, 0, unroll=8)
    ang = cos_s[...]
    low = lax.broadcasted_iota(jnp.int32, ang.shape, 1) < 64
    sin_t = jnp.sin(ang)
    sin_s[...] = jnp.where(low, -sin_t, sin_t)
    cos_s[...] = jnp.cos(ang)

    for c in small:
        c.wait()

    def ln_body(i, carry):
        r = pl.ds(pl.multiple_of(i * LN_ROWS, LN_ROWS), LN_ROWS)
        xf = x_s[r, :].astype(F32)
        mean = jnp.mean(xf, axis=-1, keepdims=True)
        cen = xf - mean
        var = jnp.mean(cen * cen, axis=-1, keepdims=True)
        nrm = cen * lax.rsqrt(var + LN_EPS)
        attn_s[r, :] = (nrm * vec_s[0:1, :] + vec_s[1:2, :]).astype(BF16)
        mlp_s[r, :] = (nrm * vec_s[2:3, :] + vec_s[3:4, :]).astype(BF16)
        return carry

    lax.fori_loop(0, rows // LN_ROWS, ln_body, 0)

    for c in range(n_chunk):
        wq_copy(c).wait()
        wqf_s[...] = wq_s[c].astype(F32)
        lhs = attn_s[:, c * QKV_CHUNK:(c + 1) * QKV_CHUNK]
        for pair in range(lines // 2):
            w = jnp.concatenate([wqf_s[pl.ds(2 * pair + e, QKV_CHUNK, stride=lines), :].astype(BF16) for e in range(2)], axis=1)
            part = jnp.dot(lhs, w, preferred_element_type=F32)
            if c == 0:
                acc_s[:, pair * 256:(pair + 1) * 256] = part
            else:
                acc_s[:, pair * 256:(pair + 1) * 256] += part

    n_slot = lines // 2
    n_q = n_slot - 2
    for j in range(n_slot):
        for g in range(2):
            col = (2 * j + g) * 128
            u = acc_s[:, col:col + 128].astype(BF16).astype(F32)
            if j < n_q + 1:
                u = (u * cos_s[...] + pltpu.roll(u, 64, 1) * sin_s[...]).astype(BF16).astype(F32)
            if j < n_q:
                q_s[pl.ds((g * n_q + j) * rows, rows), :] = u
            else:
                kv_s[pl.ds(((j - n_q) * 2 + g) * rows, rows), :] = u

    slot_ids = lax.broadcasted_iota(jnp.int32, (8, 256), 1)
    tile_ids = lax.broadcasted_iota(jnp.int32, (16, 128), 0)
    first = lax.broadcasted_iota(jnp.int32, (8, 128), 0) < 4
    scale = 128 ** -0.5

    def attend_block(i, slot):
        pos = [pos_ref[i * ROW_BLOCK + r] for r in range(ROW_BLOCK)]
        for r in range(ROW_BLOCK):
            base = pl.multiple_of((pos[r] // 16) * 16, 16)
            hit = tile_ids == pos[r] - base
            b = i * ROW_BLOCK + r
            for g in range(2):
                for buf, which in ((kbuf, 0), (vbuf, 1)):
                    new = kv_s[pl.ds((which * 2 + g) * rows + b, 1), :]
                    old = buf[slot, r, g, pl.ds(base, 16), :].astype(F32)
                    buf[slot, r, g, pl.ds(base, 16), :] = jnp.where(hit, new, old).astype(BF16)
        scores = []
        for r in range(ROW_BLOCK):
            b = i * ROW_BLOCK + r
            q = q_s[pl.ds(b, 8, stride=rows), :]
            zero = jnp.zeros_like(q)
            q2 = jnp.concatenate([jnp.where(first, q, zero), jnp.where(first, zero, q)], axis=1).astype(BF16)
            k2 = jnp.concatenate([kbuf[slot, r, 0], kbuf[slot, r, 1]], axis=1)
            s = lax.dot_general(q2, k2, (((1,), (1,)), ((), ())), preferred_element_type=F32) * scale
            scores.append(jnp.where(slot_ids <= pos[r], s, NEG_BIG))
        s = jnp.concatenate(scores, axis=0)
        e = jnp.exp(s - jnp.max(s, axis=-1, keepdims=True))
        p = (e / jnp.sum(e, axis=-1, keepdims=True)).astype(BF16)
        for r in range(ROW_BLOCK):
            v2 = jnp.concatenate([vbuf[slot, r, 0], vbuf[slot, r, 1]], axis=1)
            c = jnp.dot(p[8 * r:8 * r + 8], v2, preferred_element_type=F32)
            ctx_s[pl.ds(i * ROW_BLOCK + r, 8, stride=rows), :] = jnp.where(first, c[:, :128], c[:, 128:])

    def hid_copy(i):
        cols = pl.ds(pl.multiple_of(i * up_cols, up_cols), up_cols)
        return pltpu.make_async_copy(hid_s.at[:, cols], hid_hbm.at[:, cols], out_sem.at[0])

    def body(i, carry):
        for s in range(SUB_BLOCKS):
            nxt = i * SUB_BLOCKS + s + KV_AHEAD

            @pl.when(nxt < n_blk)
            def _():
                nslot = lax.rem(nxt, KV_SLOTS)

                @pl.when(nxt >= KV_SLOTS)
                def _():
                    wait_out(nslot)
                start_in(nxt, nslot)

        @pl.when((i >= 1) & (i - 1 + UP_SLOTS < n_up))
        def _():
            up_copy(i - 1 + UP_SLOTS, lax.rem(i - 1, UP_SLOTS)).start()

        uslot = lax.rem(i, UP_SLOTS)
        up_copy(0, uslot).wait()
        pre = jnp.dot(mlp_s[...], up_s[uslot], preferred_element_type=F32)
        act = 0.5 * pre * (1.0 + lax.erf(pre * (0.5 ** 0.5)))
        hid_s[:, pl.ds(pl.multiple_of(i * up_cols, up_cols), up_cols)] = act.astype(BF16)
        for s in range(SUB_BLOCKS):
            blk = i * SUB_BLOCKS + s
            slot = lax.rem(blk, KV_SLOTS)
            wait_in(slot)
            attend_block(blk, slot)
            start_out(blk, slot)
        hid_copy(i).start()
        return carry

    lax.fori_loop(0, n_up, body, 0)
    ctx_out = pltpu.make_async_copy(ctx_s, ctx_hbm, out_sem.at[1])
    ctx_out.start()
    pltpu.make_async_copy(hid_s, hid_hbm, out_sem.at[0]).wait()
    ctx_out.wait()
    for i in range(n_blk - KV_SLOTS, n_blk):
        wait_out(i % KV_SLOTS)


def front(pos, x, ga, ba, gm, bm, freq, wq, wu, kc, vc):
    rows, width = x.shape
    hid = wu.shape[1]
    lines = wq.shape[0] // width
    n_head = (lines // 2 - 2) * 2
    up_cols = hid // (rows // (ROW_BLOCK * SUB_BLOCKS))
    return pl.pallas_call(
        front_kernel,
        name='front',
        in_specs=[SMEM] + [ANY] * 10,
        out_specs=[ANY] * 4,
        out_shape=[
            jax.ShapeDtypeStruct(kc.shape, BF16),
            jax.ShapeDtypeStruct(vc.shape, BF16),
            jax.ShapeDtypeStruct((rows, hid), BF16),
            jax.ShapeDtypeStruct((n_head * rows, 128), F32),
        ],
        scratch_shapes=[
            pltpu.VMEM((rows, width), BF16),
            pltpu.VMEM((4, width), F32),
            pltpu.VMEM((1, 128), F32),
            pltpu.VMEM((rows, 128), F32),
            pltpu.VMEM((rows, 128), F32),
            pltpu.VMEM((rows, width), BF16),
            pltpu.VMEM((rows, width), BF16),
            pltpu.VMEM((width // QKV_CHUNK, QKV_CHUNK * lines, 128), BF16),
            pltpu.VMEM((QKV_CHUNK * lines, 128), F32),
            pltpu.VMEM((rows, lines * 128), F32),
            pltpu.VMEM((n_head * rows, 128), F32),
            pltpu.VMEM((4 * rows, 128), F32),
            pltpu.VMEM((UP_SLOTS, width, up_cols), BF16),
            pltpu.VMEM((rows, hid), BF16),
            pltpu.VMEM((n_head * rows, 128), F32),
            pltpu.VMEM((KV_SLOTS, ROW_BLOCK) + kc.shape[1:], BF16),
            pltpu.VMEM((KV_SLOTS, ROW_BLOCK) + vc.shape[1:], BF16),
            pltpu.SemaphoreType.DMA((6,)),
            pltpu.SemaphoreType.DMA((width // QKV_CHUNK,)),
            pltpu.SemaphoreType.DMA((UP_SLOTS,)),
            pltpu.SemaphoreType.DMA((KV_SLOTS,)),
            pltpu.SemaphoreType.DMA((KV_SLOTS,)),
            pltpu.SemaphoreType.DMA((KV_SLOTS,)),
            pltpu.SemaphoreType.DMA((KV_SLOTS,)),
            pltpu.SemaphoreType.DMA((2,)),
        ],
        compiler_params=pltpu.CompilerParams(vmem_limit_bytes=63 * MIB),
        cost_estimate=pl.CostEstimate(flops=22 * 10 ** 9, bytes_accessed=180 * 10 ** 6, transcendentals=0),
    )(pos, x, ga, ba, gm, bm, freq, wq, wu, kc, vc)


PIECES = 8
MESH = pl.DeviceIdType.MESH


def exchange_kernel(x_hbm, hid_hbm, ctx_hbm, wd_hbm, wo_hbm, out_hbm,
                    x_s, hid_s, ctx_s, lhs_s, wd_s, wo_s, send_s, recv_s, keep_s, sum_s, other_s, out_s,
                    in_sem, wd_sem, wo_sem, c1_send, c1_recv, c2_send, c2_recv, c3_send, c3_recv, out_sem):
    rows, width = x_s.shape
    half = width // 2
    cols = half // PIECES
    heads = ctx_s.shape[0] // rows
    me = lax.axis_index('tp')
    core = lax.rem(me, 2)
    mate = me + 1 - 2 * core
    far = lax.rem(me + 2, 4)

    loads = [pltpu.make_async_copy(a, b, in_sem.at[i]) for i, (a, b) in enumerate(((hid_hbm, hid_s), (ctx_hbm, ctx_s), (x_hbm, x_s)))]
    for c in loads[:2]:
        c.start()

    def col_of(p, part):
        side = core if part else 1 - core
        return pl.multiple_of(side * half + p * cols, cols)

    def wd_copy(p, part):
        return pltpu.make_async_copy(wd_hbm.at[:, pl.ds(col_of(p, part), cols)], wd_s.at[2 * p + part], wd_sem.at[2 * p + part])

    def wo_copy(p, part):
        return pltpu.make_async_copy(wo_hbm.at[:, pl.ds(col_of(p, part), cols)], wo_s.at[2 * p + part], wo_sem.at[2 * p + part])

    for p in range(PIECES):
        for part in range(2):
            wd_copy(p, part).start()
            wo_copy(p, part).start()
        if p == 0:
            loads[2].start()

    barrier = pltpu.get_barrier_semaphore()
    for peer in (mate, far):
        pl.semaphore_signal(barrier, inc=1, device_id={'tp': peer}, device_id_type=MESH)
    pl.semaphore_wait(barrier, 2)

    def copy1(p):
        return pltpu.make_async_remote_copy(send_s.at[p], recv_s.at[p], c1_send.at[p], c1_recv.at[p], device_id={'tp': mate}, device_id_type=MESH)

    def copy2(p):
        return pltpu.make_async_remote_copy(sum_s.at[p], other_s.at[p], c2_send.at[p], c2_recv.at[p], device_id={'tp': far}, device_id_type=MESH)

    def copy3(p, side):
        view = out_s.at[side * PIECES + p]
        return pltpu.make_async_remote_copy(view, view, c3_send.at[p], c3_recv.at[p], device_id={'tp': mate}, device_id_type=MESH)

    loads[0].wait()
    loads[1].wait()
    for h in range(heads):
        lhs_s[:, h * 128:(h + 1) * 128] = ctx_s[h * rows:(h + 1) * rows, :].astype(BF16)

    def partial(p, part):
        wd_copy(p, part).wait()
        wo_copy(p, part).wait()
        return jnp.dot(lhs_s[...], wo_s[2 * p + part], preferred_element_type=F32) + jnp.dot(hid_s[...], wd_s[2 * p + part], preferred_element_type=F32)

    def chip_sum(p):
        copy1(p).wait_recv()
        sum_s[p] = (keep_s[p] + recv_s[p].astype(F32)).astype(BF16)
        copy2(p).start()

    def compute(p, carry):
        send_s[p] = partial(p, 0).astype(BF16)
        copy1(p).start()
        keep_s[p] = partial(p, 1)
        chip_sum(p)
        return carry

    lax.fori_loop(0, PIECES, compute, 0)
    loads[2].wait()

    def out_copy(p, side):
        k = side * PIECES + p
        return pltpu.make_async_copy(out_s.at[k], out_hbm.at[:, pl.ds(pl.multiple_of(k * cols, cols), cols)], out_sem.at[k])

    def finish(p, carry):
        copy2(p).wait_recv()
        xs = x_s[:, pl.ds(col_of(p, 1), cols)].astype(F32)
        out_s[core * PIECES + p] = (xs + (sum_s[p].astype(F32) + other_s[p].astype(F32))).astype(BF16)
        copy3(p, core).start()
        out_copy(p, core).start()
        return carry

    lax.fori_loop(0, PIECES, finish, 0)

    def collect(p, carry):
        copy3(p, 1 - core).wait_recv()
        out_copy(p, 1 - core).start()
        return carry

    lax.fori_loop(0, PIECES, collect, 0)

    def drain(p, carry):
        copy1(p).wait_send()
        copy2(p).wait_send()
        copy3(p, core).wait_send()
        out_copy(p, core).wait()
        out_copy(p, 1 - core).wait()
        return carry

    lax.fori_loop(0, PIECES, drain, 0)


def exchange(x, hid, ctx, wd, wo):
    rows, width = x.shape
    cols = width // 2 // PIECES
    n_ff = hid.shape[1]
    n_ctx = wo.shape[0]
    dma = pltpu.SemaphoreType.DMA
    return pl.pallas_call(
        exchange_kernel,
        name='exchange',
        in_specs=[ANY] * 5,
        out_specs=ANY,
        out_shape=jax.ShapeDtypeStruct((rows, width), BF16),
        scratch_shapes=[
            pltpu.VMEM((rows, width), BF16),
            pltpu.VMEM((rows, n_ff), BF16),
            pltpu.VMEM(ctx.shape, F32),
            pltpu.VMEM((rows, n_ctx), BF16),
            pltpu.VMEM((2 * PIECES, n_ff, cols), BF16),
            pltpu.VMEM((2 * PIECES, n_ctx, cols), BF16),
            pltpu.VMEM((PIECES, rows, cols), BF16),
            pltpu.VMEM((PIECES, rows, cols), BF16),
            pltpu.VMEM((PIECES, rows, cols), F32),
            pltpu.VMEM((PIECES, rows, cols), BF16),
            pltpu.VMEM((PIECES, rows, cols), BF16),
            pltpu.VMEM((2 * PIECES, rows, cols), BF16),
            dma((3,)), dma((2 * PIECES,)), dma((2 * PIECES,)),
            dma((PIECES,)), dma((PIECES,)), dma((PIECES,)), dma((PIECES,)), dma((PIECES,)), dma((PIECES,)),
            dma((2 * PIECES,)),
        ],
        compiler_params=pltpu.CompilerParams(vmem_limit_bytes=63 * MIB, collective_id=0, has_side_effects=True),
        cost_estimate=pl.CostEstimate(flops=11 * 10 ** 9, bytes_accessed=48 * 10 ** 6, transcendentals=0),
    )(x, hid, ctx, wd, wo)


def solution(mesh):
    row_spec = P('dp', None)
    vec_spec = P(None)
    cache_spec = P('dp', 'tp', None, None)

    def device_step(x, ln_attn_gamma, ln_attn_beta, ln_mlp_gamma, ln_mlp_beta, w_qkv, w_out, w_up, w_down, k_cache, v_cache, positions):
        width = x.shape[1]
        head = w_qkv.shape[3]
        inv_freq = ROPE_BASE ** (-2.0 * np.arange(head // 2) / head)
        freq = jnp.asarray(np.concatenate([inv_freq, inv_freq])[None, :], F32)
        vecs = [v.reshape(1, width) for v in (ln_attn_gamma, ln_attn_beta, ln_mlp_gamma, ln_mlp_beta)]
        wq = jnp.transpose(w_qkv, (0, 2, 1, 3)).reshape(-1, head)
        ko, vo, hid, ctx = front(positions, x, *vecs, freq, wq, w_up, k_cache, v_cache)
        out = exchange(x, hid, ctx, w_down, w_out.reshape(-1, width))
        return out, ko, vo

    return jax.shard_map(device_step, mesh=mesh, in_specs=(row_spec, vec_spec, vec_spec, vec_spec, vec_spec, P(None, 'tp', None, None), P('tp', None, None, None), P(None, 'tp'), P('tp', None), cache_spec, cache_spec, P('dp')), out_specs=(row_spec, cache_spec, cache_spec), check_vma=False)
```

time: 270 us -> 124 us (0.46)
  Pallas kernels: 0 us -> 120 us
  matrix products: 84 us -> 0 us
  waiting for transfers between devices: 82.7 us -> 0 us
  other arithmetic: 55.5 us -> 0 us
  local copies, waits for them, and re-layouts: 32.3 us -> 3.13 us
  between operations: 14.2 us -> 0.65 us
    pallas_call x0 -> x2, Pallas kernels: none -> 120 us  [the longest x1 74.3 us: front(): pl.pallas_call(front_kernel, name='front', in_specs=[SMEM] + [ANY] * 10,...]
    psum x1 -> x0, waiting for transfers between devices: 82.7 us -> none  [device_step(): mlp_total = lax.psum(mlp_part, 'tp')]
    dot_general x4 -> x0, matrix products: 61 us -> none  [the longest x1 23.7 us: device_step(): jnp.dot(mlp_in, w_up, preferred_element_type=jnp.float32)]
    select_n x1 -> x0, other arithmetic: 43.7 us -> none  [attend_local(): keys_all = jnp.where(write_mask, new_key[:, :, None, :], k_cache)]
    unnamed x13 -> x1, local copies, waits for them, and re-layouts: 31.1 us -> 3.13 us
    sub x1 -> x0, matrix products: 16.3 us -> none  [attend_local(): attn_probs = jax.nn.softmax(scores, axis=-1).astype(jnp.bfloat16)]
    unnamed x1 -> x0, matrix products: 6.77 us -> none
    convert_element_type x5 -> x0, other arithmetic: 5.51 us -> none  [the longest x1 4.62 us: device_step(): (x.astype(jnp.float32) + attn_total.astype(jnp.float32) + mlp_total.astyp...]
  transfers between devices with their start and end apart: 1 -> 0, of which waited for: 1 -> 0; matrix products, arithmetic and copies ran while one was open for 0% -> 0% of each run, Pallas kernels for 0% -> 0%
where the time goes in v2:
time: 124 us
  Pallas kernels  120 us (97%)
  local copies, waits for them, and re-layouts  3.13 us (3%)
    pallas_call x1, Pallas kernels, front(): pl.pallas_call(front_kernel, name='front', in_specs=[SMEM] + [ANY] * 10,...  74.3 us
    pallas_call x1, Pallas kernels, exchange(): pl.pallas_call(exchange_kernel, name='exchange', in_specs=[ANY] * 5, out_...  45.8 us
    unnamed x1, local copies, waits for them, and re-layouts  3.13 us

profile of v2, /device:TPU:0, one launch (start us, length us, event | category | flops | bytes accessed | tf_op | source)
XLA Modules:
  0.0 123.9 jit_solution(9266482244811407446)
XLA Ops:
  0.6 74.3 %front.1 = (bf16[256,2,256,128]{3,2,1,0:T(8,128)(2,1)}, bf16[256,2,256,128]{3,2,1,0:T(8,128)(2,1)}, bf16[256,4096]{1,0:T(8,128)(2,1)}, f32[2048,128]{1,0:T(8,128)}) custom-call(s32[256]{0:T(256)} %pos_ref.1, bf16[256,4096]{1,0:T(8,128)(2,1)} %x_hbm.3, f32[1,4096]{1,0:T(1,128)} %bitcast.10, f32[1,4096]{1,0:T(1,128)} %bitcast.11, f32[1,4096]{1,0:T(1,128)} %bitcast.12, ...), custom_call_target="tpu_custom_call" | custom-call | flops 22000001024 | bytes 180000000 | tf_op jit(solution)/shard_map/front/pallas_call | solution.py:215
  74.9 45.8 %exchange.1 = bf16[256,4096]{1,0:T(8,128)(2,1)} custom-call(bf16[256,4096]{1,0:T(8,128)(2,1)} %x_hbm.3, bf16[256,4096]{1,0:T(8,128)(2,1)} %get-tuple-element.7.hid_hbm, f32[2048,128]{1,0:T(8,128)} %get-tuple-element.8.ctx_hbm, bf16[4096,4096]{1,0:T(8,128)(2,1)} %wd_hbm.1, bf16[1024,4096]{1,0:T(8,128)(2,1)} %bitcast.9), custom_call_target="tpu_custom_call" | custom-call | flops 11000000512 | bytes 48000000 | tf_op jit(solution)/shard_map/exchange/pallas_call | solution.py:373
  120.8 3.1 %copy.17 = bf16[256,4096]{1,0:T(8,128)(2,1)} copy(bf16[256,4096]{1,0:T(8,128)(2,1)} %exchange.1) | data formatting | bytes 4194304

commit v3 on v2

--- a/solution.py
+++ b/solution.py
@@ -68,12 +68,8 @@
         pltpu.make_async_copy(kbuf.at[slot], block(ko_hbm, 0), kout_sem.at[slot]).wait()
         pltpu.make_async_copy(vbuf.at[slot], block(vo_hbm, 0), vout_sem.at[slot]).wait()
 
-    for c in range(n_chunk):
-        wq_copy(c).start()
-    for b in range(UP_SLOTS):
-        up_copy(b, b).start()
-    for i in range(KV_AHEAD):
-        start_in(i, i)
+    wq_copy(0).start()
+    wq_copy(1).start()
 
     freq_in.wait()
 
@@ -90,6 +86,8 @@
 
     for c in small:
         c.wait()
+    wq_copy(2).start()
+    wq_copy(3).start()
 
     def ln_body(i, carry):
         r = pl.ds(pl.multiple_of(i * LN_ROWS, LN_ROWS), LN_ROWS)
@@ -102,10 +100,17 @@
         mlp_s[r, :] = (nrm * vec_s[2:3, :] + vec_s[3:4, :]).astype(BF16)
         return carry
 
-    lax.fori_loop(0, rows // LN_ROWS, ln_body, 0)
+    half_ln = rows // LN_ROWS // 2
+    lax.fori_loop(0, half_ln, ln_body, 0)
+    for c in range(4, n_chunk):
+        wq_copy(c).start()
+    lax.fori_loop(half_ln, 2 * half_ln, ln_body, 0)
 
     for c in range(n_chunk):
         wq_copy(c).wait()
+        start_in(c, c)
+        if c >= n_chunk - UP_SLOTS:
+            up_copy(c - n_chunk + UP_SLOTS, c - n_chunk + UP_SLOTS).start()
         wqf_s[...] = wq_s[c].astype(F32)
         lhs = attn_s[:, c * QKV_CHUNK:(c + 1) * QKV_CHUNK]
         for pair in range(lines // 2):
@@ -256,6 +261,7 @@
 
 
 PIECES = 8
+W_SLOTS = 4
 MESH = pl.DeviceIdType.MESH
 
 
@@ -279,18 +285,21 @@
         side = core if part else 1 - core
         return pl.multiple_of(side * half + p * cols, cols)
 
+    def slot_of(p, part):
+        return (2 * p + part) % W_SLOTS
+
     def wd_copy(p, part):
-        return pltpu.make_async_copy(wd_hbm.at[:, pl.ds(col_of(p, part), cols)], wd_s.at[2 * p + part], wd_sem.at[2 * p + part])
+        return pltpu.make_async_copy(wd_hbm.at[:, pl.ds(col_of(p, part), cols)], wd_s.at[slot_of(p, part)], wd_sem.at[slot_of(p, part)])
 
     def wo_copy(p, part):
-        return pltpu.make_async_copy(wo_hbm.at[:, pl.ds(col_of(p, part), cols)], wo_s.at[2 * p + part], wo_sem.at[2 * p + part])
-
-    for p in range(PIECES):
-        for part in range(2):
-            wd_copy(p, part).start()
-            wo_copy(p, part).start()
-        if p == 0:
-            loads[2].start()
+        return pltpu.make_async_copy(wo_hbm.at[:, pl.ds(col_of(p, part), cols)], wo_s.at[slot_of(p, part)], wo_sem.at[slot_of(p, part)])
+
+    def w_start(p, part):
+        wd_copy(p, part).start()
+        wo_copy(p, part).start()
+
+    w_start(0, 0)
+    w_start(0, 1)
 
     barrier = pltpu.get_barrier_semaphore()
     for peer in (mate, far):
@@ -307,6 +316,8 @@
         view = out_s.at[side * PIECES + p]
         return pltpu.make_async_remote_copy(view, view, c3_send.at[p], c3_recv.at[p], device_id={'tp': mate}, device_id_type=MESH)
 
+    w_start(1, 0)
+    loads[2].start()
     loads[0].wait()
     loads[1].wait()
     for h in range(heads):
@@ -315,7 +326,13 @@
     def partial(p, part):
         wd_copy(p, part).wait()
         wo_copy(p, part).wait()
-        return jnp.dot(lhs_s[...], wo_s[2 * p + part], preferred_element_type=F32) + jnp.dot(hid_s[...], wd_s[2 * p + part], preferred_element_type=F32)
+        nxt = p + 1 + part
+
+        @pl.when(nxt < PIECES)
+        def _():
+            w_start(nxt, 1 - part)
+        slot = slot_of(p, part)
+        return jnp.dot(lhs_s[...], wo_s[slot], preferred_element_type=F32) + jnp.dot(hid_s[...], wd_s[slot], preferred_element_type=F32)
 
     def chip_sum(p):
         copy1(p).wait_recv()
@@ -381,15 +398,15 @@
             pltpu.VMEM((rows, n_ff), BF16),
             pltpu.VMEM(ctx.shape, F32),
             pltpu.VMEM((rows, n_ctx), BF16),
-            pltpu.VMEM((2 * PIECES, n_ff, cols), BF16),
-            pltpu.VMEM((2 * PIECES, n_ctx, cols), BF16),
+            pltpu.VMEM((W_SLOTS, n_ff, cols), BF16),
+            pltpu.VMEM((W_SLOTS, n_ctx, cols), BF16),
             pltpu.VMEM((PIECES, rows, cols), BF16),
             pltpu.VMEM((PIECES, rows, cols), BF16),
             pltpu.VMEM((PIECES, rows, cols), F32),
             pltpu.VMEM((PIECES, rows, cols), BF16),
             pltpu.VMEM((PIECES, rows, cols), BF16),
             pltpu.VMEM((2 * PIECES, rows, cols), BF16),
-            dma((3,)), dma((2 * PIECES,)), dma((2 * PIECES,)),
+            dma((3,)), dma((W_SLOTS,)), dma((W_SLOTS,)),
             dma((PIECES,)), dma((PIECES,)), dma((PIECES,)), dma((PIECES,)), dma((PIECES,)), dma((PIECES,)),
             dma((2 * PIECES,)),
         ],

time: 124 us -> 107 us (0.86)
  Pallas kernels: 120 us -> 103 us
    pallas_call x1, Pallas kernels: 45.8 us -> 35.7 us  [exchange(): pl.pallas_call(exchange_kernel, name='exchange', in_specs=[ANY] * 5, out_...]
    pallas_call x1, Pallas kernels: 74.3 us -> 67.1 us  [front(): pl.pallas_call(front_kernel, name='front', in_specs=[SMEM] + [ANY] * 10,...]
where the time goes in v3:
time: 107 us
  Pallas kernels  103 us (96%)
  local copies, waits for them, and re-layouts  3.13 us (3%)
    pallas_call x1, Pallas kernels, front(): pl.pallas_call(front_kernel, name='front', in_specs=[SMEM] + [ANY] * 10,...  67.1 us
    pallas_call x1, Pallas kernels, exchange(): pl.pallas_call(exchange_kernel, name='exchange', in_specs=[ANY] * 5, out_...  35.7 us
    unnamed x1, local copies, waits for them, and re-layouts  3.13 us

profile of v3, /device:TPU:0, one launch (start us, length us, event | category | flops | bytes accessed | tf_op | source)
XLA Modules:
  0.0 106.6 jit_solution(13500095717561184187)
XLA Ops:
  0.6 67.1 %front.1 = (bf16[256,2,256,128]{3,2,1,0:T(8,128)(2,1)}, bf16[256,2,256,128]{3,2,1,0:T(8,128)(2,1)}, bf16[256,4096]{1,0:T(8,128)(2,1)}, f32[2048,128]{1,0:T(8,128)}) custom-call(s32[256]{0:T(256)} %pos_ref.1, bf16[256,4096]{1,0:T(8,128)(2,1)} %x_hbm.3, f32[1,4096]{1,0:T(1,128)} %bitcast.10, f32[1,4096]{1,0:T(1,128)} %bitcast.11, f32[1,4096]{1,0:T(1,128)} %bitcast.12, ...), custom_call_target="tpu_custom_call" | custom-call | flops 22000001024 | bytes 180000000 | tf_op jit(solution)/shard_map/front/pallas_call | solution.py:220
  67.7 35.7 %exchange.1 = bf16[256,4096]{1,0:T(8,128)(2,1)} custom-call(bf16[256,4096]{1,0:T(8,128)(2,1)} %x_hbm.3, bf16[256,4096]{1,0:T(8,128)(2,1)} %get-tuple-element.7.hid_hbm, f32[2048,128]{1,0:T(8,128)} %get-tuple-element.8.ctx_hbm, bf16[4096,4096]{1,0:T(8,128)(2,1)} %wd_hbm.1, bf16[1024,4096]{1,0:T(8,128)(2,1)} %bitcast.9), custom_call_target="tpu_custom_call" | custom-call | flops 11000000512 | bytes 48000000 | tf_op jit(solution)/shard_map/exchange/pallas_call | solution.py:390
  103.4 3.1 %copy.17 = bf16[256,4096]{1,0:T(8,128)(2,1)} copy(bf16[256,4096]{1,0:T(8,128)(2,1)} %exchange.1) | data formatting | bytes 4194304

commit v4 on v3

--- a/solution.py
+++ b/solution.py
@@ -12,6 +12,7 @@
 BF16 = jnp.bfloat16
 F32 = jnp.float32
 ANY = pl.BlockSpec(memory_space=pl.ANY)
+HBM = pl.BlockSpec(memory_space=pltpu.HBM)
 SMEM = pl.BlockSpec(memory_space=pltpu.SMEM)
 MIB = 1024 * 1024
 
@@ -19,9 +20,10 @@
 LN_ROWS = 16
 ROW_BLOCK = 8
 SUB_BLOCKS = 2
-KV_SLOTS = 12
-KV_AHEAD = 8
-UP_SLOTS = 3
+KV_SLOTS = 10
+KV_AHEAD = 6
+UP_SLOTS = 4
+W_PARTS = 4
 
 
 def front_kernel(pos_ref, x_hbm, ga_hbm, ba_hbm, gm_hbm, bm_hbm, freq_hbm, wq_hbm, wu_hbm, kc_hbm, vc_hbm,
@@ -46,15 +48,21 @@
     def wq_copy(c):
         return pltpu.make_async_copy(wq_hbm.at[pl.ds(c * QKV_CHUNK * lines, QKV_CHUNK * lines), :], wq_s.at[c], wq_sem.at[c])
 
-    def up_copy(b, slot):
-        return pltpu.make_async_copy(wu_hbm.at[:, pl.ds(pl.multiple_of(b * up_cols, up_cols), up_cols)], up_s.at[slot], up_sem.at[slot])
+    def up_start(b, slot):
+        cols = pl.ds(pl.multiple_of(b * up_cols, up_cols), up_cols)
+        for k in range(W_PARTS):
+            part = pl.ds(k * (width // W_PARTS), width // W_PARTS)
+            pltpu.make_async_copy(wu_hbm.at[part, cols], up_s.at[slot, part, :], up_sem.at[slot]).start()
+
+    def up_wait(slot):
+        pltpu.make_async_copy(wu_hbm.at[:, pl.ds(0, up_cols)], up_s.at[slot], up_sem.at[slot]).wait()
 
     def block(ref, i):
         return ref.at[pl.ds(i * ROW_BLOCK, ROW_BLOCK)]
 
     def start_in(i, slot):
-        pltpu.make_async_copy(block(kc_hbm, i), kbuf.at[slot], kin_sem.at[slot]).start()
-        pltpu.make_async_copy(block(vc_hbm, i), vbuf.at[slot], vin_sem.at[slot]).start()
+        pltpu.make_async_copy(block(kc_hbm, i), kbuf.at[slot], kin_sem.at[slot]).start(priority=1)
+        pltpu.make_async_copy(block(vc_hbm, i), vbuf.at[slot], vin_sem.at[slot]).start(priority=1)
 
     def wait_in(slot):
         pltpu.make_async_copy(block(kc_hbm, 0), kbuf.at[slot], kin_sem.at[slot]).wait()
@@ -108,9 +116,10 @@
 
     for c in range(n_chunk):
         wq_copy(c).wait()
-        start_in(c, c)
+        if c < KV_AHEAD:
+            start_in(c, c)
         if c >= n_chunk - UP_SLOTS:
-            up_copy(c - n_chunk + UP_SLOTS, c - n_chunk + UP_SLOTS).start()
+            up_start(c - n_chunk + UP_SLOTS, c - n_chunk + UP_SLOTS)
         wqf_s[...] = wq_s[c].astype(F32)
         lhs = attn_s[:, c * QKV_CHUNK:(c + 1) * QKV_CHUNK]
         for pair in range(lines // 2):
@@ -186,10 +195,10 @@
 
         @pl.when((i >= 1) & (i - 1 + UP_SLOTS < n_up))
         def _():
-            up_copy(i - 1 + UP_SLOTS, lax.rem(i - 1, UP_SLOTS)).start()
+            up_start(i - 1 + UP_SLOTS, lax.rem(i - 1, UP_SLOTS))
 
         uslot = lax.rem(i, UP_SLOTS)
-        up_copy(0, uslot).wait()
+        up_wait(uslot)
         pre = jnp.dot(mlp_s[...], up_s[uslot], preferred_element_type=F32)
         act = 0.5 * pre * (1.0 + lax.erf(pre * (0.5 ** 0.5)))
         hid_s[:, pl.ds(pl.multiple_of(i * up_cols, up_cols), up_cols)] = act.astype(BF16)
@@ -220,8 +229,8 @@
     return pl.pallas_call(
         front_kernel,
         name='front',
-        in_specs=[SMEM] + [ANY] * 10,
-        out_specs=[ANY] * 4,
+        in_specs=[SMEM] + [HBM] * 10,
+        out_specs=[HBM] * 4,
         out_shape=[
             jax.ShapeDtypeStruct(kc.shape, BF16),
             jax.ShapeDtypeStruct(vc.shape, BF16),
@@ -265,9 +274,9 @@
 MESH = pl.DeviceIdType.MESH
 
 
-def exchange_kernel(x_hbm, hid_hbm, ctx_hbm, wd_hbm, wo_hbm, out_hbm,
-                    x_s, hid_s, ctx_s, lhs_s, wd_s, wo_s, send_s, recv_s, keep_s, sum_s, other_s, out_s,
-                    in_sem, wd_sem, wo_sem, c1_send, c1_recv, c2_send, c2_recv, c3_send, c3_recv, out_sem):
+def exchange_kernel(x_hbm, hid_hbm, ctx_hbm, wd_hbm, wo_hbm, out_ref,
+                    x_s, hid_s, ctx_s, lhs_s, wd_s, wo_s, send_s, recv_s, keep_s, sum_s, other_s,
+                    in_sem, wd_sem, wo_sem, c1_send, c1_recv, c2_send, c2_recv, c3_send, c3_recv):
     rows, width = x_s.shape
     half = width // 2
     cols = half // PIECES
@@ -278,8 +287,10 @@
     far = lax.rem(me + 2, 4)
 
     loads = [pltpu.make_async_copy(a, b, in_sem.at[i]) for i, (a, b) in enumerate(((hid_hbm, hid_s), (ctx_hbm, ctx_s), (x_hbm, x_s)))]
-    for c in loads[:2]:
-        c.start()
+    loads[1].start()
+    for k in range(W_PARTS):
+        part = pl.ds(k * (rows // W_PARTS), rows // W_PARTS)
+        pltpu.make_async_copy(hid_hbm.at[part, :], hid_s.at[part, :], in_sem.at[0]).start()
 
     def col_of(p, part):
         side = core if part else 1 - core
@@ -288,18 +299,20 @@
     def slot_of(p, part):
         return (2 * p + part) % W_SLOTS
 
-    def wd_copy(p, part):
-        return pltpu.make_async_copy(wd_hbm.at[:, pl.ds(col_of(p, part), cols)], wd_s.at[slot_of(p, part)], wd_sem.at[slot_of(p, part)])
+    def wd_copy(p, part, k=None):
+        depth = wd_hbm.shape[0] // W_PARTS
+        rng = slice(None) if k is None else pl.ds(k * depth, depth)
+        return pltpu.make_async_copy(wd_hbm.at[rng, pl.ds(col_of(p, part), cols)], wd_s.at[slot_of(p, part), rng, :], wd_sem.at[slot_of(p, part)])
 
     def wo_copy(p, part):
         return pltpu.make_async_copy(wo_hbm.at[:, pl.ds(col_of(p, part), cols)], wo_s.at[slot_of(p, part)], wo_sem.at[slot_of(p, part)])
 
     def w_start(p, part):
-        wd_copy(p, part).start()
         wo_copy(p, part).start()
+        for k in range(W_PARTS):
+            wd_copy(p, part, k).start()
 
     w_start(0, 0)
-    w_start(0, 1)
 
     barrier = pltpu.get_barrier_semaphore()
     for peer in (mate, far):
@@ -313,15 +326,16 @@
         return pltpu.make_async_remote_copy(sum_s.at[p], other_s.at[p], c2_send.at[p], c2_recv.at[p], device_id={'tp': far}, device_id_type=MESH)
 
     def copy3(p, side):
-        view = out_s.at[side * PIECES + p]
+        view = out_ref.at[:, pl.ds(pl.multiple_of(side * half + p * cols, cols), cols)]
         return pltpu.make_async_remote_copy(view, view, c3_send.at[p], c3_recv.at[p], device_id={'tp': mate}, device_id_type=MESH)
 
+    loads[1].wait()
+    w_start(0, 1)
+    for h in range(heads):
+        lhs_s[:, h * 128:(h + 1) * 128] = ctx_s[h * rows:(h + 1) * rows, :].astype(BF16)
+    loads[0].wait()
     w_start(1, 0)
     loads[2].start()
-    loads[0].wait()
-    loads[1].wait()
-    for h in range(heads):
-        lhs_s[:, h * 128:(h + 1) * 128] = ctx_s[h * rows:(h + 1) * rows, :].astype(BF16)
 
     def partial(p, part):
         wd_copy(p, part).wait()
@@ -349,33 +363,20 @@
     lax.fori_loop(0, PIECES, compute, 0)
     loads[2].wait()
 
-    def out_copy(p, side):
-        k = side * PIECES + p
-        return pltpu.make_async_copy(out_s.at[k], out_hbm.at[:, pl.ds(pl.multiple_of(k * cols, cols), cols)], out_sem.at[k])
-
     def finish(p, carry):
         copy2(p).wait_recv()
         xs = x_s[:, pl.ds(col_of(p, 1), cols)].astype(F32)
-        out_s[core * PIECES + p] = (xs + (sum_s[p].astype(F32) + other_s[p].astype(F32))).astype(BF16)
+        out_ref[:, pl.ds(col_of(p, 1), cols)] = (xs + (sum_s[p].astype(F32) + other_s[p].astype(F32))).astype(BF16)
         copy3(p, core).start()
-        out_copy(p, core).start()
         return carry
 
     lax.fori_loop(0, PIECES, finish, 0)
-
-    def collect(p, carry):
-        copy3(p, 1 - core).wait_recv()
-        out_copy(p, 1 - core).start()
-        return carry
-
-    lax.fori_loop(0, PIECES, collect, 0)
 
     def drain(p, carry):
         copy1(p).wait_send()
         copy2(p).wait_send()
         copy3(p, core).wait_send()
-        out_copy(p, core).wait()
-        out_copy(p, 1 - core).wait()
+        copy3(p, 1 - core).wait_recv()
         return carry
 
     lax.fori_loop(0, PIECES, drain, 0)
@@ -390,8 +391,8 @@
     return pl.pallas_call(
         exchange_kernel,
         name='exchange',
-        in_specs=[ANY] * 5,
-        out_specs=ANY,
+        in_specs=[HBM] * 5,
+        out_specs=pl.BlockSpec(memory_space=pltpu.VMEM),
         out_shape=jax.ShapeDtypeStruct((rows, width), BF16),
         scratch_shapes=[
             pltpu.VMEM((rows, width), BF16),
@@ -405,12 +406,10 @@
             pltpu.VMEM((PIECES, rows, cols), F32),
             pltpu.VMEM((PIECES, rows, cols), BF16),
             pltpu.VMEM((PIECES, rows, cols), BF16),
-            pltpu.VMEM((2 * PIECES, rows, cols), BF16),
             dma((3,)), dma((W_SLOTS,)), dma((W_SLOTS,)),
             dma((PIECES,)), dma((PIECES,)), dma((PIECES,)), dma((PIECES,)), dma((PIECES,)), dma((PIECES,)),
-            dma((2 * PIECES,)),
         ],
-        compiler_params=pltpu.CompilerParams(vmem_limit_bytes=63 * MIB, collective_id=0, has_side_effects=True),
+        compiler_params=pltpu.CompilerParams(vmem_limit_bytes=32 * MIB, collective_id=0, has_side_effects=True),
         cost_estimate=pl.CostEstimate(flops=11 * 10 ** 9, bytes_accessed=48 * 10 ** 6, transcendentals=0),
     )(x, hid, ctx, wd, wo)
 
@@ -428,7 +427,8 @@
         vecs = [v.reshape(1, width) for v in (ln_attn_gamma, ln_attn_beta, ln_mlp_gamma, ln_mlp_beta)]
         wq = jnp.transpose(w_qkv, (0, 2, 1, 3)).reshape(-1, head)
         ko, vo, hid, ctx = front(positions, x, *vecs, freq, wq, w_up, k_cache, v_cache)
-        out = exchange(x, hid, ctx, w_down, w_out.reshape(-1, width))
+        held = [pltpu.with_memory_space_constraint(a, pltpu.HBM) for a in (x, hid, ctx, w_down, w_out.reshape(-1, width))]
+        out = exchange(*held)
         return out, ko, vo
 
     return jax.shard_map(device_step, mesh=mesh, in_specs=(row_spec, vec_spec, vec_spec, vec_spec, vec_spec, P(None, 'tp', None, None), P('tp', None, None, None), P(None, 'tp'), P('tp', None), cache_spec, cache_spec, P('dp')), out_specs=(row_spec, cache_spec, cache_spec), check_vma=False)

time: 107 us -> 103 us (0.963)
  Pallas kernels: 103 us -> 101 us
  local copies, waits for them, and re-layouts: 3.13 us -> 1.32 us
    unnamed x1, local copies, waits for them, and re-layouts: 3.13 us -> 1.32 us
    pallas_call x2, Pallas kernels: 103 us -> 101 us  [the longest x1 65.6 us: front(): pl.pallas_call(front_kernel, name='front', in_specs=[SMEM] + [HBM] * 10,...]
where the time goes in v4:
time: 103 us
  Pallas kernels  101 us (98%)
  local copies, waits for them, and re-layouts  1.32 us (1%)
    pallas_call x1, Pallas kernels, front(): pl.pallas_call(front_kernel, name='front', in_specs=[SMEM] + [HBM] * 10,...  65.6 us
    pallas_call x1, Pallas kernels, exchange(): pl.pallas_call(exchange_kernel, name='exchange', in_specs=[HBM] * 5, out_...  35.4 us

profile of v4, /device:TPU:0, one launch (start us, length us, event | category | flops | bytes accessed | tf_op | source)
XLA Modules:
  0.0 103.0 jit_solution(3271074075299011558)
XLA Ops:
  0.6 65.6 %front.1 = (bf16[256,2,256,128]{3,2,1,0:T(8,128)(2,1)}, bf16[256,2,256,128]{3,2,1,0:T(8,128)(2,1)}, bf16[256,4096]{1,0:T(8,128)(2,1)}, f32[2048,128]{1,0:T(8,128)}) custom-call(s32[256]{0:T(256)} %pos_ref.1, bf16[256,4096]{1,0:T(8,128)(2,1)} %x_hbm.3, f32[1,4096]{1,0:T(1,128)} %bitcast.10, f32[1,4096]{1,0:T(1,128)} %bitcast.11, f32[1,4096]{1,0:T(1,128)} %bitcast.12, ...), custom_call_target="tpu_custom_call" | custom-call | flops 22000001024 | bytes 180000000 | tf_op jit(solution)/shard_map/front/pallas_call | solution.py:229
  66.3 35.4 %exchange.1 = bf16[256,4096]{1,0:T(8,128)(2,1)S(1)} custom-call(bf16[256,4096]{1,0:T(8,128)(2,1)} %x_hbm.3, bf16[256,4096]{1,0:T(8,128)(2,1)} %get-tuple-element.7.hid_hbm, f32[2048,128]{1,0:T(8,128)} %get-tuple-element.8.ctx_hbm, bf16[4096,4096]{1,0:T(8,128)(2,1)} %wd_hbm.1, bf16[1024,4096]{1,0:T(8,128)(2,1)} %bitcast.9), custom_call_target="tpu_custom_call" | custom-call | flops 11000000512 | bytes 48000000 | tf_op jit(solution)/shard_map/exchange/pallas_call | solution.py:391
  101.7 1.3 %copy.17 = bf16[256,4096]{1,0:T(8,128)(2,1)} copy(bf16[256,4096]{1,0:T(8,128)(2,1)S(1)} %exchange.1) | data formatting | bytes 4194304

commit v5 on v4

--- a/solution.py
+++ b/solution.py
@@ -199,15 +199,19 @@
 
         uslot = lax.rem(i, UP_SLOTS)
         up_wait(uslot)
-        pre = jnp.dot(mlp_s[...], up_s[uslot], preferred_element_type=F32)
+        for s in range(SUB_BLOCKS):
+            wait_in(lax.rem(i * SUB_BLOCKS + s, KV_SLOTS))
+        deep = width // 2
+        pre = (jnp.dot(mlp_s[:, :deep], up_s[uslot, :deep, :], preferred_element_type=F32)
+               + jnp.dot(mlp_s[:, deep:], up_s[uslot, deep:, :], preferred_element_type=F32))
         act = 0.5 * pre * (1.0 + lax.erf(pre * (0.5 ** 0.5)))
         hid_s[:, pl.ds(pl.multiple_of(i * up_cols, up_cols), up_cols)] = act.astype(BF16)
         for s in range(SUB_BLOCKS):
             blk = i * SUB_BLOCKS + s
-            slot = lax.rem(blk, KV_SLOTS)
-            wait_in(slot)
-            attend_block(blk, slot)
-            start_out(blk, slot)
+            attend_block(blk, lax.rem(blk, KV_SLOTS))
+        for s in range(SUB_BLOCKS):
+            blk = i * SUB_BLOCKS + s
+            start_out(blk, lax.rem(blk, KV_SLOTS))
         hid_copy(i).start()
         return carry
 
@@ -269,50 +273,51 @@
     )(pos, x, ga, ba, gm, bm, freq, wq, wu, kc, vc)
 
 
-PIECES = 8
+PIECES = 16
 W_SLOTS = 4
 MESH = pl.DeviceIdType.MESH
 
 
 def exchange_kernel(x_hbm, hid_hbm, ctx_hbm, wd_hbm, wo_hbm, out_ref,
-                    x_s, hid_s, ctx_s, lhs_s, wd_s, wo_s, send_s, recv_s, keep_s, sum_s, other_s,
-                    in_sem, wd_sem, wo_sem, c1_send, c1_recv, c2_send, c2_recv, c3_send, c3_recv):
+                    x_s, ctx_s, lhs_s, w_s, send_s, recv_s, keep_s, sum_s, other_s,
+                    in_sem, w_sem, c1_send, c1_recv, c2_send, c2_recv, c3_send, c3_recv):
     rows, width = x_s.shape
     half = width // 2
     cols = half // PIECES
     heads = ctx_s.shape[0] // rows
+    n_ff, n_ctx = wd_hbm.shape[0], wo_hbm.shape[0]
     me = lax.axis_index('tp')
     core = lax.rem(me, 2)
     mate = me + 1 - 2 * core
     far = lax.rem(me + 2, 4)
 
-    loads = [pltpu.make_async_copy(a, b, in_sem.at[i]) for i, (a, b) in enumerate(((hid_hbm, hid_s), (ctx_hbm, ctx_s), (x_hbm, x_s)))]
-    loads[1].start()
+    ctx_in = pltpu.make_async_copy(ctx_hbm, ctx_s, in_sem.at[1])
+    ctx_in.start()
     for k in range(W_PARTS):
         part = pl.ds(k * (rows // W_PARTS), rows // W_PARTS)
-        pltpu.make_async_copy(hid_hbm.at[part, :], hid_s.at[part, :], in_sem.at[0]).start()
+        pltpu.make_async_copy(hid_hbm.at[part, :], lhs_s.at[part, pl.ds(0, n_ff)], in_sem.at[0]).start()
 
     def col_of(p, part):
         side = core if part else 1 - core
         return pl.multiple_of(side * half + p * cols, cols)
 
-    def slot_of(p, part):
-        return (2 * p + part) % W_SLOTS
-
-    def wd_copy(p, part, k=None):
-        depth = wd_hbm.shape[0] // W_PARTS
-        rng = slice(None) if k is None else pl.ds(k * depth, depth)
-        return pltpu.make_async_copy(wd_hbm.at[rng, pl.ds(col_of(p, part), cols)], wd_s.at[slot_of(p, part), rng, :], wd_sem.at[slot_of(p, part)])
-
-    def wo_copy(p, part):
-        return pltpu.make_async_copy(wo_hbm.at[:, pl.ds(col_of(p, part), cols)], wo_s.at[slot_of(p, part)], wo_sem.at[slot_of(p, part)])
-
-    def w_start(p, part):
-        wo_copy(p, part).start()
-        for k in range(W_PARTS):
-            wd_copy(p, part, k).start()
-
-    w_start(0, 0)
+    def w_start(p):
+        slot = lax.rem(p, W_SLOTS)
+        for part in range(2):
+            src, dst = pl.ds(col_of(p, part), cols), pl.ds(part * cols, cols)
+            pltpu.make_async_copy(wo_hbm.at[:, src], w_s.at[slot, pl.ds(n_ff, n_ctx), dst], w_sem.at[slot]).start()
+            for k in range(2):
+                deep = pl.ds(k * (n_ff // 2), n_ff // 2)
+                pltpu.make_async_copy(wd_hbm.at[deep, src], w_s.at[slot, deep, dst], w_sem.at[slot]).start()
+
+    def w_wait(p):
+        slot = lax.rem(p, W_SLOTS)
+        for part in range(2):
+            dst = pl.ds(part * cols, cols)
+            pltpu.make_async_copy(wo_hbm.at[:, pl.ds(0, cols)], w_s.at[slot, pl.ds(n_ff, n_ctx), dst], w_sem.at[slot]).wait()
+            pltpu.make_async_copy(wd_hbm.at[:, pl.ds(0, cols)], w_s.at[slot, pl.ds(0, n_ff), dst], w_sem.at[slot]).wait()
+
+    w_start(0)
 
     barrier = pltpu.get_barrier_semaphore()
     for peer in (mate, far):
@@ -329,24 +334,14 @@
         view = out_ref.at[:, pl.ds(pl.multiple_of(side * half + p * cols, cols), cols)]
         return pltpu.make_async_remote_copy(view, view, c3_send.at[p], c3_recv.at[p], device_id={'tp': mate}, device_id_type=MESH)
 
-    loads[1].wait()
-    w_start(0, 1)
+    ctx_in.wait()
+    w_start(1)
     for h in range(heads):
-        lhs_s[:, h * 128:(h + 1) * 128] = ctx_s[h * rows:(h + 1) * rows, :].astype(BF16)
-    loads[0].wait()
-    w_start(1, 0)
-    loads[2].start()
-
-    def partial(p, part):
-        wd_copy(p, part).wait()
-        wo_copy(p, part).wait()
-        nxt = p + 1 + part
-
-        @pl.when(nxt < PIECES)
-        def _():
-            w_start(nxt, 1 - part)
-        slot = slot_of(p, part)
-        return jnp.dot(lhs_s[...], wo_s[slot], preferred_element_type=F32) + jnp.dot(hid_s[...], wd_s[slot], preferred_element_type=F32)
+        lhs_s[:, n_ff + h * 128:n_ff + (h + 1) * 128] = ctx_s[h * rows:(h + 1) * rows, :].astype(BF16)
+    pltpu.make_async_copy(hid_hbm, lhs_s.at[:, pl.ds(0, n_ff)], in_sem.at[0]).wait()
+    x_in = pltpu.make_async_copy(x_hbm, x_s, in_sem.at[2])
+    x_in.start()
+    w_start(2)
 
     def chip_sum(p):
         copy1(p).wait_recv()
@@ -354,14 +349,27 @@
         copy2(p).start()
 
     def compute(p, carry):
-        send_s[p] = partial(p, 0).astype(BF16)
+        w_wait(p)
+
+        @pl.when(p + 3 < PIECES)
+        def _():
+            w_start(p + 3)
+        slot = lax.rem(p, W_SLOTS)
+        deep = (n_ff + n_ctx) // 2
+        s = (jnp.dot(lhs_s[:, :deep], w_s[slot, :deep, :], preferred_element_type=F32)
+             + jnp.dot(lhs_s[:, deep:], w_s[slot, deep:, :], preferred_element_type=F32))
+        send_s[p] = s[:, :cols].astype(BF16)
+        keep_s[p] = s[:, cols:]
         copy1(p).start()
-        keep_s[p] = partial(p, 1)
-        chip_sum(p)
+
+        @pl.when(p > 0)
+        def _():
+            chip_sum(p - 1)
         return carry
 
     lax.fori_loop(0, PIECES, compute, 0)
-    loads[2].wait()
+    chip_sum(PIECES - 1)
+    x_in.wait()
 
     def finish(p, carry):
         copy2(p).wait_recv()
@@ -396,17 +404,15 @@
         out_shape=jax.ShapeDtypeStruct((rows, width), BF16),
         scratch_shapes=[
             pltpu.VMEM((rows, width), BF16),
-            pltpu.VMEM((rows, n_ff), BF16),
             pltpu.VMEM(ctx.shape, F32),
-            pltpu.VMEM((rows, n_ctx), BF16),
-            pltpu.VMEM((W_SLOTS, n_ff, cols), BF16),
-            pltpu.VMEM((W_SLOTS, n_ctx, cols), BF16),
+            pltpu.VMEM((rows, n_ff + n_ctx), BF16),
+            pltpu.VMEM((W_SLOTS, n_ff + n_ctx, 2 * cols), BF16),
             pltpu.VMEM((PIECES, rows, cols), BF16),
             pltpu.VMEM((PIECES, rows, cols), BF16),
             pltpu.VMEM((PIECES, rows, cols), F32),
             pltpu.VMEM((PIECES, rows, cols), BF16),
             pltpu.VMEM((PIECES, rows, cols), BF16),
-            dma((3,)), dma((W_SLOTS,)), dma((W_SLOTS,)),
+            dma((3,)), dma((W_SLOTS,)),
             dma((PIECES,)), dma((PIECES,)), dma((PIECES,)), dma((PIECES,)), dma((PIECES,)), dma((PIECES,)),
         ],
         compiler_params=pltpu.CompilerParams(vmem_limit_bytes=32 * MIB, collective_id=0, has_side_effects=True),

time: 103 us -> 98.8 us (0.959)
  Pallas kernels: 101 us -> 96.7 us
    pallas_call x1, Pallas kernels: 65.6 us -> 63.4 us  [front(): pl.pallas_call(front_kernel, name='front', in_specs=[SMEM] + [HBM] * 10,...]
    pallas_call x1, Pallas kernels: 35.4 us -> 33.3 us  [exchange(): pl.pallas_call(exchange_kernel, name='exchange', in_specs=[HBM] * 5, out_...]
where the time goes in v5:
time: 98.8 us; the launch traced here: 98.7 us
  Pallas kernels  96.7 us (98%)
  local copies, waits for them, and re-layouts  1.32 us (1%)
    pallas_call x1, Pallas kernels, front(): pl.pallas_call(front_kernel, name='front', in_specs=[SMEM] + [HBM] * 10,...  63.4 us
    pallas_call x1, Pallas kernels, exchange(): pl.pallas_call(exchange_kernel, name='exchange', in_specs=[HBM] * 5, out_...  33.3 us

profile of v5, /device:TPU:0, one launch (start us, length us, event | category | flops | bytes accessed | tf_op | source)
XLA Modules:
  0.0 98.7 jit_solution(10240000054478582529)
XLA Ops:
  0.6 63.4 %front.1 = (bf16[256,2,256,128]{3,2,1,0:T(8,128)(2,1)}, bf16[256,2,256,128]{3,2,1,0:T(8,128)(2,1)}, bf16[256,4096]{1,0:T(8,128)(2,1)}, f32[2048,128]{1,0:T(8,128)}) custom-call(s32[256]{0:T(256)} %pos_ref.1, bf16[256,4096]{1,0:T(8,128)(2,1)} %x_hbm.3, f32[1,4096]{1,0:T(1,128)} %bitcast.10, f32[1,4096]{1,0:T(1,128)} %bitcast.11, f32[1,4096]{1,0:T(1,128)} %bitcast.12, ...), custom_call_target="tpu_custom_call" | custom-call | flops 22000001024 | bytes 180000000 | tf_op jit(solution)/shard_map/front/pallas_call | solution.py:233
  64.1 33.3 %exchange.1 = bf16[256,4096]{1,0:T(8,128)(2,1)S(1)} custom-call(bf16[256,4096]{1,0:T(8,128)(2,1)} %x_hbm.3, bf16[256,4096]{1,0:T(8,128)(2,1)} %get-tuple-element.7.hid_hbm, f32[2048,128]{1,0:T(8,128)} %get-tuple-element.8.ctx_hbm, bf16[4096,4096]{1,0:T(8,128)(2,1)} %wd_hbm.1, bf16[1024,4096]{1,0:T(8,128)(2,1)} %bitcast.9), custom_call_target="tpu_custom_call" | custom-call | flops 11000000512 | bytes 48000000 | tf_op jit(solution)/shard_map/exchange/pallas_call | solution.py:399
  97.4 1.3 %copy.17 = bf16[256,4096]{1,0:T(8,128)(2,1)} copy(bf16[256,4096]{1,0:T(8,128)(2,1)S(1)} %exchange.1) | data formatting | bytes 4194304

commit v6 on v5

v6 whole, which is shorter than its diff:
```python
import jax
import jax.numpy as jnp
import numpy as np
from jax import lax
from jax.experimental import pallas as pl
from jax.experimental.pallas import tpu as pltpu
from jax.sharding import PartitionSpec as P

LN_EPS = 1e-5
ROPE_BASE = 10000.0
NEG_BIG = -1e30
BF16 = jnp.bfloat16
F32 = jnp.float32
ANY = pl.BlockSpec(memory_space=pl.ANY)
HBM = pl.BlockSpec(memory_space=pltpu.HBM)
VMEM = pl.BlockSpec(memory_space=pltpu.VMEM)
SMEM = pl.BlockSpec(memory_space=pltpu.SMEM)
MIB = 1024 * 1024

QKV_CHUNK = 512
LN_ROWS = 16
ROW_BLOCK = 8
SUB_BLOCKS = 2
KV_SLOTS = 12
KV_AHEAD = 8
UP_SLOTS = 4
W_PARTS = 4


def front_kernel(pos_ref, x_hbm, ga_hbm, ba_hbm, gm_hbm, bm_hbm, freq_hbm, wq_hbm, wu_hbm, wd_hbm, wo_hbm, kc_hbm, vc_hbm,
                 ko_hbm, vo_hbm, lhs_ref, w0_ref,
                 x_s, vec_s, freq_s, cos_s, sin_s, attn_s, wqf_s, acc_s, q_s, kv_s, up_s, ctx_s, kbuf, vbuf,
                 in_sem, wq_sem, up_sem, kin_sem, vin_sem, kout_sem, vout_sem, w0_sem):
    mlp_s = x_s
    rows, width = x_s.shape
    seq = kc_hbm.shape[0] // (2 * rows)
    lines_blk = ROW_BLOCK * 2 * seq
    n_ff = lhs_ref.shape[1] - wo_hbm.shape[0]
    n_chunk = width // QKV_CHUNK
    lines = wq_hbm.shape[0] // width
    up_cols = up_s.shape[2]
    n_up = wu_hbm.shape[1] // up_cols
    n_blk = rows // ROW_BLOCK

    small = [pltpu.make_async_copy(x_hbm, x_s, in_sem.at[0])]
    for i, v in enumerate((ga_hbm, ba_hbm, gm_hbm, bm_hbm)):
        small.append(pltpu.make_async_copy(v, vec_s.at[pl.ds(i, 1), :], in_sem.at[1 + i]))
    freq_in = pltpu.make_async_copy(freq_hbm, freq_s, in_sem.at[5])
    freq_in.start()
    for c in small:
        c.start()

    wq_lines = QKV_CHUNK * lines
    wq_base = (KV_SLOTS - n_chunk * wq_lines // (2 * lines_blk)) * lines_blk
    wq_order = [c for pair in zip(range(n_chunk // 2), range(n_chunk // 2, n_chunk)) for c in pair]

    def wq_view(c):
        buf = kbuf if c < n_chunk // 2 else vbuf
        return buf.at[pl.ds(wq_base + (c % (n_chunk // 2)) * wq_lines, wq_lines), :]

    def wq_copy(c):
        return pltpu.make_async_copy(wq_hbm.at[pl.ds(c * wq_lines, wq_lines), :], wq_view(c), wq_sem.at[c])

    def up_start(b, slot):
        cols = pl.ds(pl.multiple_of(b * up_cols, up_cols), up_cols)
        for k in range(W_PARTS):
            part = pl.ds(k * (width // W_PARTS), width // W_PARTS)
            pltpu.make_async_copy(wu_hbm.at[part, cols], up_s.at[slot, part, :], up_sem.at[slot]).start()

    def up_wait(slot):
        pltpu.make_async_copy(wu_hbm.at[:, pl.ds(0, up_cols)], up_s.at[slot], up_sem.at[slot]).wait()

    def block(ref, i):
        return ref.at[pl.ds(pl.multiple_of(i * lines_blk, lines_blk), lines_blk), :]

    def start_in(i, slot):
        pltpu.make_async_copy(block(kc_hbm, i), block(kbuf, slot), kin_sem.at[slot]).start(priority=1)
        pltpu.make_async_copy(block(vc_hbm, i), block(vbuf, slot), vin_sem.at[slot]).start(priority=1)

    def wait_in(slot):
        pltpu.make_async_copy(block(kc_hbm, 0), block(kbuf, slot), kin_sem.at[slot]).wait()
        pltpu.make_async_copy(block(vc_hbm, 0), block(vbuf, slot), vin_sem.at[slot]).wait()

    def start_out(i, slot):
        pltpu.make_async_copy(block(kbuf, slot), block(ko_hbm, i), kout_sem.at[slot]).start()
        pltpu.make_async_copy(block(vbuf, slot), block(vo_hbm, i), vout_sem.at[slot]).start()

    def wait_out(slot):
        pltpu.make_async_copy(block(kbuf, slot), block(ko_hbm, 0), kout_sem.at[slot]).wait()
        pltpu.make_async_copy(block(vbuf, slot), block(vo_hbm, 0), vout_sem.at[slot]).wait()

    for c in wq_order[:2]:
        wq_copy(c).start()

    freq_in.wait()

    def angle_body(b, carry):
        cos_s[pl.ds(b, 1), :] = pos_ref[b].astype(F32) * freq_s[0:1, :]
        return carry

    lax.fori_loop(0, rows, angle_body, 0, unroll=8)
    ang = cos_s[...]
    low = lax.broadcasted_iota(jnp.int32, ang.shape, 1) < 64
    sin_t = jnp.sin(ang)
    sin_s[...] = jnp.where(low, -sin_t, sin_t)
    cos_s[...] = jnp.cos(ang)

    for c in small:
        c.wait()
    for c in wq_order[2:4]:
        wq_copy(c).start()

    def ln_body(i, carry):
        r = pl.ds(pl.multiple_of(i * LN_ROWS, LN_ROWS), LN_ROWS)
        xf = x_s[r, :].astype(F32)
        mean = jnp.mean(xf, axis=-1, keepdims=True)
        cen = xf - mean
        var = jnp.mean(cen * cen, axis=-1, keepdims=True)
        nrm = cen * lax.rsqrt(var + LN_EPS)
        attn_s[r, :] = (nrm * vec_s[0:1, :] + vec_s[1:2, :]).astype(BF16)
        mlp_s[r, :] = (nrm * vec_s[2:3, :] + vec_s[3:4, :]).astype(BF16)
        return carry

    half_ln = rows // LN_ROWS // 2
    lax.fori_loop(0, half_ln, ln_body, 0)
    for c in wq_order[4:]:
        wq_copy(c).start()
    lax.fori_loop(half_ln, 2 * half_ln, ln_body, 0)

    for step, c in enumerate(wq_order):
        wq_copy(c).wait()
        if step < KV_AHEAD:
            start_in(step, step)
        if step >= n_chunk - UP_SLOTS:
            up_start(step - n_chunk + UP_SLOTS, step - n_chunk + UP_SLOTS)
        wqf_s[...] = wq_view(c)[...].astype(F32)
        lhs = attn_s[:, c * QKV_CHUNK:(c + 1) * QKV_CHUNK]
        for pair in range(lines // 2):
            w = jnp.concatenate([wqf_s[pl.ds(2 * pair + e, QKV_CHUNK, stride=lines), :].astype(BF16) for e in range(2)], axis=1)
            part = jnp.dot(lhs, w, preferred_element_type=F32)
            if step == 0:
                acc_s[:, pair * 256:(pair + 1) * 256] = part
            else:
                acc_s[:, pair * 256:(pair + 1) * 256] += part

    n_slot = lines // 2
    n_q = n_slot - 2
    for j in range(n_slot):
        for g in range(2):
            col = (2 * j + g) * 128
            u = acc_s[:, col:col + 128].astype(BF16).astype(F32)
            if j < n_q + 1:
                u = (u * cos_s[...] + pltpu.roll(u, 64, 1) * sin_s[...]).astype(BF16).astype(F32)
            if j < n_q:
                q_s[pl.ds((g * n_q + j) * rows, rows), :] = u
            else:
                kv_s[pl.ds(((j - n_q) * 2 + g) * rows, rows), :] = u

    slot_ids = lax.broadcasted_iota(jnp.int32, (8, 256), 1)
    tile_ids = lax.broadcasted_iota(jnp.int32, (16, 128), 0)
    first = lax.broadcasted_iota(jnp.int32, (8, 128), 0) < 4
    scale = 128 ** -0.5

    def pair_of(buf, slot, r):
        at = [pl.ds(pl.multiple_of(slot * lines_blk + (2 * r + g) * seq, seq), seq) for g in range(2)]
        return jnp.concatenate([buf[a, :] for a in at], axis=1)

    def attend_block(i, slot):
        pos = [pos_ref[i * ROW_BLOCK + r] for r in range(ROW_BLOCK)]
        for r in range(ROW_BLOCK):
            base = pl.multiple_of((pos[r] // 16) * 16, 16)
            hit = tile_ids == pos[r] - base
            b = i * ROW_BLOCK + r
            for g in range(2):
                tile = pl.ds(pl.multiple_of(slot * lines_blk + (2 * r + g) * seq + base, 16), 16)
                for buf, which in ((kbuf, 0), (vbuf, 1)):
                    new = kv_s[pl.ds((which * 2 + g) * rows + b, 1), :]
                    buf[tile, :] = jnp.where(hit, new, buf[tile, :].astype(F32)).astype(BF16)
        scores = []
        for r in range(ROW_BLOCK):
            b = i * ROW_BLOCK + r
            q = q_s[pl.ds(b, 8, stride=rows), :]
            zero = jnp.zeros_like(q)
            q2 = jnp.concatenate([jnp.where(first, q, zero), jnp.where(first, zero, q)], axis=1).astype(BF16)
            k2 = pair_of(kbuf, slot, r)
            s = lax.dot_general(q2, k2, (((1,), (1,)), ((), ())), preferred_element_type=F32) * scale
            scores.append(jnp.where(slot_ids <= pos[r], s, NEG_BIG))
        s = jnp.concatenate(scores, axis=0)
        e = jnp.exp(s - jnp.max(s, axis=-1, keepdims=True))
        p = (e / jnp.sum(e, axis=-1, keepdims=True)).astype(BF16)
        for r in range(ROW_BLOCK):
            v2 = pair_of(vbuf, slot, r)
            c = jnp.dot(p[8 * r:8 * r + 8], v2, preferred_element_type=F32)
            ctx_s[pl.ds(i * ROW_BLOCK + r, 8, stride=rows), :] = jnp.where(first, c[:, :128], c[:, 128:])

    core = lax.rem(lax.axis_index('tp'), 2)
    cols = w0_ref.shape[1] // 2
    w0_in = []
    for part in range(2):
        src = pl.ds(pl.multiple_of((core if part else 1 - core) * (wd_hbm.shape[1] // 2), cols), cols)
        dst = pl.ds(part * cols, cols)
        w0_in.append(pltpu.make_async_copy(wd_hbm.at[:, src], w0_ref.at[pl.ds(0, n_ff), dst], w0_sem.at[0]))
        w0_in.append(pltpu.make_async_copy(wo_hbm.at[:, src], w0_ref.at[pl.ds(n_ff, wo_hbm.shape[0]), dst], w0_sem.at[0]))

    def body(i, carry):
        for s in range(SUB_BLOCKS):
            nxt = i * SUB_BLOCKS + s + KV_AHEAD

            @pl.when(nxt < n_blk)
            def _():
                nslot = lax.rem(nxt, KV_SLOTS)

                @pl.when(nxt >= KV_SLOTS)
                def _():
                    wait_out(nslot)
                start_in(nxt, nslot)

        @pl.when((i >= 1) & (i - 1 + UP_SLOTS < n_up))
        def _():
            up_start(i - 1 + UP_SLOTS, lax.rem(i - 1, UP_SLOTS))

        uslot = lax.rem(i, UP_SLOTS)
        up_wait(uslot)
        for s in range(SUB_BLOCKS):
            wait_in(lax.rem(i * SUB_BLOCKS + s, KV_SLOTS))
        deep = width // 2
        pre = (jnp.dot(mlp_s[:, :deep], up_s[uslot, :deep, :], preferred_element_type=F32)
               + jnp.dot(mlp_s[:, deep:], up_s[uslot, deep:, :], preferred_element_type=F32))
        act = 0.5 * pre * (1.0 + lax.erf(pre * (0.5 ** 0.5)))
        lhs_ref[:, pl.ds(pl.multiple_of(i * up_cols, up_cols), up_cols)] = act.astype(BF16)
        for s in range(SUB_BLOCKS):
            blk = i * SUB_BLOCKS + s
            attend_block(blk, lax.rem(blk, KV_SLOTS))
        for s in range(SUB_BLOCKS):
            blk = i * SUB_BLOCKS + s
            start_out(blk, lax.rem(blk, KV_SLOTS))

        @pl.when(i == n_up - 4)
        def _():
            for c in w0_in:
                c.start(priority=1)
        return carry

    lax.fori_loop(0, n_up, body, 0)
    for h in range(ctx_s.shape[0] // rows):
        lhs_ref[:, n_ff + h * 128:n_ff + (h + 1) * 128] = ctx_s[h * rows:(h + 1) * rows, :].astype(BF16)
    for c in w0_in:
        c.wait()
    for i in range(n_blk - KV_SLOTS, n_blk):
        wait_out(i % KV_SLOTS)


def front(pos, x, ga, ba, gm, bm, freq, wq, wu, wd, wo, kc, vc):
    rows, width = x.shape
    hid = wu.shape[1]
    lines = wq.shape[0] // width
    n_head = (lines // 2 - 2) * 2
    up_cols = hid // (rows // (ROW_BLOCK * SUB_BLOCKS))
    lines_blk = kc.shape[0] // rows * ROW_BLOCK
    return pl.pallas_call(
        front_kernel,
        name='front',
        in_specs=[SMEM] + [HBM] * 12,
        out_specs=[HBM, HBM, VMEM, VMEM],
        out_shape=[
            jax.ShapeDtypeStruct(kc.shape, BF16),
            jax.ShapeDtypeStruct(vc.shape, BF16),
            jax.ShapeDtypeStruct((rows, hid + wo.shape[0]), BF16),
            jax.ShapeDtypeStruct((hid + wo.shape[0], width // PIECES), BF16),
        ],
        scratch_shapes=[
            pltpu.VMEM((rows, width), BF16),
            pltpu.VMEM((4, width), F32),
            pltpu.VMEM((1, 128), F32),
            pltpu.VMEM((rows, 128), F32),
            pltpu.VMEM((rows, 128), F32),
            pltpu.VMEM((rows, width), BF16),
            pltpu.VMEM((QKV_CHUNK * lines, 128), F32),
            pltpu.VMEM((rows, lines * 128), F32),
            pltpu.VMEM((n_head * rows, 128), F32),
            pltpu.VMEM((4 * rows, 128), F32),
            pltpu.VMEM((UP_SLOTS, width, up_cols), BF16),
            pltpu.VMEM((n_head * rows, 128), F32),
            pltpu.VMEM((KV_SLOTS * lines_blk, 128), BF16),
            pltpu.VMEM((KV_SLOTS * lines_blk, 128), BF16),
            pltpu.SemaphoreType.DMA((6,)),
            pltpu.SemaphoreType.DMA((width // QKV_CHUNK,)),
            pltpu.SemaphoreType.DMA((UP_SLOTS,)),
            pltpu.SemaphoreType.DMA((KV_SLOTS,)),
            pltpu.SemaphoreType.DMA((KV_SLOTS,)),
            pltpu.SemaphoreType.DMA((KV_SLOTS,)),
            pltpu.SemaphoreType.DMA((KV_SLOTS,)),
            pltpu.SemaphoreType.DMA((1,)),
        ],
        compiler_params=pltpu.CompilerParams(vmem_limit_bytes=44 * MIB),
        cost_estimate=pl.CostEstimate(flops=22 * 10 ** 9, bytes_accessed=180 * 10 ** 6, transcendentals=0),
    )(pos, x, ga, ba, gm, bm, freq, wq, wu, wd, wo, kc, vc)


PIECES = 16
W_SLOTS = 4
MESH = pl.DeviceIdType.MESH


def exchange_kernel(x_hbm, lhs_s, w0_ref, wd_hbm, wo_hbm, out_ref,
                    x_s, w_s, send_s, recv_s, keep_s, sum_s, other_s,
                    in_sem, w_sem, c1_send, c1_recv, c2_send, c2_recv, c3_send, c3_recv):
    rows, width = x_s.shape
    half = width // 2
    cols = half // PIECES
    n_ff, n_ctx = wd_hbm.shape[0], wo_hbm.shape[0]
    me = lax.axis_index('tp')
    core = lax.rem(me, 2)
    mate = me + 1 - 2 * core
    far = lax.rem(me + 2, 4)

    def col_of(p, part):
        side = core if part else 1 - core
        return pl.multiple_of(side * half + p * cols, cols)

    def w_start(p):
        slot = lax.rem(p, W_SLOTS)
        for part in range(2):
            src, dst = pl.ds(col_of(p, part), cols), pl.ds(part * cols, cols)
            pltpu.make_async_copy(wo_hbm.at[:, src], w_s.at[slot, pl.ds(n_ff, n_ctx), dst], w_sem.at[slot]).start()
            for k in range(2):
                deep = pl.ds(k * (n_ff // 2), n_ff // 2)
                pltpu.make_async_copy(wd_hbm.at[deep, src], w_s.at[slot, deep, dst], w_sem.at[slot]).start()

    def w_wait(p):
        slot = lax.rem(p, W_SLOTS)
        for part in range(2):
            dst = pl.ds(part * cols, cols)
            pltpu.make_async_copy(wo_hbm.at[:, pl.ds(0, cols)], w_s.at[slot, pl.ds(n_ff, n_ctx), dst], w_sem.at[slot]).wait()
            pltpu.make_async_copy(wd_hbm.at[:, pl.ds(0, cols)], w_s.at[slot, pl.ds(0, n_ff), dst], w_sem.at[slot]).wait()

    for p in range(1, W_SLOTS):
        w_start(p)
    x_in = pltpu.make_async_copy(x_hbm, x_s, in_sem.at[0])
    x_in.start()

    barrier = pltpu.get_barrier_semaphore()
    for peer in (mate, far):
        pl.semaphore_signal(barrier, inc=1, device_id={'tp': peer}, device_id_type=MESH)
    pl.semaphore_wait(barrier, 2)

    def copy1(p):
        return pltpu.make_async_remote_copy(send_s.at[p], recv_s.at[p], c1_send.at[p], c1_recv.at[p], device_id={'tp': mate}, device_id_type=MESH)

    def copy2(p):
        return pltpu.make_async_remote_copy(sum_s.at[p], other_s.at[p], c2_send.at[p], c2_recv.at[p], device_id={'tp': far}, device_id_type=MESH)

    def copy3(p, side):
        view = out_ref.at[:, pl.ds(pl.multiple_of(side * half + p * cols, cols), cols)]
        return pltpu.make_async_remote_copy(view, view, c3_send.at[p], c3_recv.at[p], device_id={'tp': mate}, device_id_type=MESH)

    def chip_sum(p):
        copy1(p).wait_recv()
        sum_s[p] = (keep_s[p] + recv_s[p].astype(F32)).astype(BF16)
        copy2(p).start()

    def partial(p, w):
        deep = (n_ff + n_ctx) // 2
        s = (jnp.dot(lhs_s[:, :deep], w[:deep, :], preferred_element_type=F32)
             + jnp.dot(lhs_s[:, deep:], w[deep:, :], preferred_element_type=F32))
        send_s[p] = s[:, :cols].astype(BF16)
        keep_s[p] = s[:, cols:]
        copy1(p).start()

    partial(0, w0_ref)
    chip_sum(0)

    def compute(p, carry):
        w_wait(p)

        @pl.when(p + 3 < PIECES)
        def _():
            w_start(p + 3)
        partial(p, w_s.at[lax.rem(p, W_SLOTS)])

        @pl.when(p > 1)
        def _():
            chip_sum(p - 1)
        return carry

    lax.fori_loop(1, PIECES, compute, 0)
    chip_sum(PIECES - 1)
    x_in.wait()

    def finish(p, carry):
        copy2(p).wait_recv()
        xs = x_s[:, pl.ds(col_of(p, 1), cols)].astype(F32)
        out_ref[:, pl.ds(col_of(p, 1), cols)] = (xs + (sum_s[p].astype(F32) + other_s[p].astype(F32))).astype(BF16)
        copy3(p, core).start()
        return carry

    lax.fori_loop(0, PIECES, finish, 0)

    def drain(p, carry):
        copy1(p).wait_send()
        copy2(p).wait_send()
        copy3(p, core).wait_send()
        copy3(p, 1 - core).wait_recv()
        return carry

    lax.fori_loop(0, PIECES, drain, 0)


def exchange(x, lhs, w0, wd, wo):
    rows, width = x.shape
    cols = width // 2 // PIECES
    n_ff = wd.shape[0]
    n_ctx = wo.shape[0]
    dma = pltpu.SemaphoreType.DMA
    return pl.pallas_call(
        exchange_kernel,
        name='exchange',
        in_specs=[HBM, VMEM, VMEM, HBM, HBM],
        out_specs=VMEM,
        out_shape=jax.ShapeDtypeStruct((rows, width), BF16),
        scratch_shapes=[
            pltpu.VMEM((rows, width), BF16),
            pltpu.VMEM((W_SLOTS, n_ff + n_ctx, 2 * cols), BF16),
            pltpu.VMEM((PIECES, rows, cols), BF16),
            pltpu.VMEM((PIECES, rows, cols), BF16),
            pltpu.VMEM((PIECES, rows, cols), F32),
            pltpu.VMEM((PIECES, rows, cols), BF16),
            pltpu.VMEM((PIECES, rows, cols), BF16),
            dma((1,)), dma((W_SLOTS,)),
            dma((PIECES,)), dma((PIECES,)), dma((PIECES,)), dma((PIECES,)), dma((PIECES,)), dma((PIECES,)),
        ],
        compiler_params=pltpu.CompilerParams(vmem_limit_bytes=32 * MIB, collective_id=0, has_side_effects=True),
        cost_estimate=pl.CostEstimate(flops=11 * 10 ** 9, bytes_accessed=48 * 10 ** 6, transcendentals=0),
    )(x, lhs, w0, wd, wo)


def solution(mesh):
    row_spec = P('dp', None)
    vec_spec = P(None)
    cache_spec = P('dp', 'tp', None, None)

    def device_step(x, ln_attn_gamma, ln_attn_beta, ln_mlp_gamma, ln_mlp_beta, w_qkv, w_out, w_up, w_down, k_cache, v_cache, positions):
        width = x.shape[1]
        head = w_qkv.shape[3]
        inv_freq = ROPE_BASE ** (-2.0 * np.arange(head // 2) / head)
        freq = jnp.asarray(np.concatenate([inv_freq, inv_freq])[None, :], F32)
        vecs = [v.reshape(1, width) for v in (ln_attn_gamma, ln_attn_beta, ln_mlp_gamma, ln_mlp_beta)]
        wq = jnp.transpose(w_qkv, (0, 2, 1, 3)).reshape(-1, head)
        wo = w_out.reshape(-1, width)
        in_hbm = [pltpu.with_memory_space_constraint(a, pltpu.HBM) for a in (positions, x, *vecs, freq, wq, w_up, w_down, wo, k_cache.reshape(-1, head), v_cache.reshape(-1, head))]
        x_h, wd_h, wo_h = in_hbm[1], in_hbm[-4], in_hbm[-3]
        ko, vo, lhs, w0 = front(*in_hbm)
        out = exchange(x_h, lhs, w0, wd_h, wo_h)
        return out, ko.reshape(k_cache.shape), vo.reshape(v_cache.shape)

    return jax.shard_map(device_step, mesh=mesh, in_specs=(row_spec, vec_spec, vec_spec, vec_spec, vec_spec, P(None, 'tp', None, None), P('tp', None, None, None), P(None, 'tp'), P('tp', None), cache_spec, cache_spec, P('dp')), out_specs=(row_spec, cache_spec, cache_spec), check_vma=False)
```

time: 98.8 us -> 95.3 us (0.965)
  Pallas kernels: 96.7 us -> 93.2 us
    pallas_call x2, Pallas kernels: 96.7 us -> 93.2 us  [the longest x1 61.9 us: front(): pl.pallas_call(front_kernel, name='front', in_specs=[SMEM] + [HBM] * 12,...]
where the time goes in v6:
time: 95.3 us; the launch traced here: 95.2 us
  Pallas kernels  93.2 us (98%)
  local copies, waits for them, and re-layouts  1.32 us (1%)
    pallas_call x1, Pallas kernels, front(): pl.pallas_call(front_kernel, name='front', in_specs=[SMEM] + [HBM] * 12,...  61.9 us
    pallas_call x1, Pallas kernels, exchange(): pl.pallas_call(exchange_kernel, name='exchange', in_specs=[HBM, VMEM, VME...  31.4 us

profile of v6, /device:TPU:0, one launch (start us, length us, event | category | flops | bytes accessed | tf_op | source)
XLA Modules:
  0.0 95.2 jit_solution(13517701935717005263)
XLA Ops:
  0.6 61.9 %front.1 = (bf16[131072,128]{1,0:T(8,128)(2,1)}, bf16[131072,128]{1,0:T(8,128)(2,1)}, bf16[256,5120]{1,0:T(8,128)(2,1)S(1)}, bf16[5120,256]{1,0:T(8,128)(2,1)S(1)}) custom-call(s32[256]{0:T(256)} %pos_ref.1, bf16[256,4096]{1,0:T(8,128)(2,1)} %x_hbm.3, f32[1,4096]{1,0:T(1,128)} %bitcast.17, f32[1,4096]{1,0:T(1,128)} %bitcast.18, f32[1,4096]{1,0:T(1,128)} %bitcast.19, ...), custom_call_target="tpu_custom_call" | custom-call | flops 22000001024 | bytes 180000000 | tf_op jit(solution)/shard_map/front/pallas_call | solution.py:260
  62.5 31.4 %exchange.1 = bf16[256,4096]{1,0:T(8,128)(2,1)S(1)} custom-call(bf16[256,4096]{1,0:T(8,128)(2,1)} %x_hbm.3, bf16[256,5120]{1,0:T(8,128)(2,1)S(1)} %get-tuple-element.7.lhs_s, bf16[5120,256]{1,0:T(8,128)(2,1)S(1)} %get-tuple-element.8.w0_ref, bf16[4096,4096]{1,0:T(8,128)(2,1)} %wd_hbm.3, bf16[1024,4096]{1,0:T(8,128)(2,1)} %bitcast.15), custom_call_target="tpu_custom_call" | custom-call | flops 11000000512 | bytes 48000000 | tf_op jit(solution)/shard_map/exchange/pallas_call | solution.py:415
  93.9 1.3 %copy.17 = bf16[256,4096]{1,0:T(8,128)(2,1)} copy(bf16[256,4096]{1,0:T(8,128)(2,1)S(1)} %exchange.1) | data formatting | bytes 4194304

commit v7 on v6

--- a/solution.py
+++ b/solution.py
@@ -42,7 +42,8 @@
     n_up = wu_hbm.shape[1] // up_cols
     n_blk = rows // ROW_BLOCK
 
-    small = [pltpu.make_async_copy(x_hbm, x_s, in_sem.at[0])]
+    x_parts = [pl.ds(k * (rows // W_PARTS), rows // W_PARTS) for k in range(W_PARTS)]
+    small = [pltpu.make_async_copy(x_hbm.at[part, :], x_s.at[part, :], in_sem.at[0]) for part in x_parts]
     for i, v in enumerate((ga_hbm, ba_hbm, gm_hbm, bm_hbm)):
         small.append(pltpu.make_async_copy(v, vec_s.at[pl.ds(i, 1), :], in_sem.at[1 + i]))
     freq_in = pltpu.make_async_copy(freq_hbm, freq_s, in_sem.at[5])
@@ -91,6 +92,8 @@
 
     for c in wq_order[:2]:
         wq_copy(c).start()
+    for i in range(2):
+        start_in(i, i)
 
     freq_in.wait()
 
@@ -109,6 +112,8 @@
         c.wait()
     for c in wq_order[2:4]:
         wq_copy(c).start()
+    for i in range(2, 4):
+        start_in(i, i)
 
     def ln_body(i, carry):
         r = pl.ds(pl.multiple_of(i * LN_ROWS, LN_ROWS), LN_ROWS)
@@ -125,11 +130,13 @@
     lax.fori_loop(0, half_ln, ln_body, 0)
     for c in wq_order[4:]:
         wq_copy(c).start()
+    for i in range(4, 6):
+        start_in(i, i)
     lax.fori_loop(half_ln, 2 * half_ln, ln_body, 0)
 
     for step, c in enumerate(wq_order):
         wq_copy(c).wait()
-        if step < KV_AHEAD:
+        if 6 <= step < KV_AHEAD:
             start_in(step, step)
         if step >= n_chunk - UP_SLOTS:
             up_start(step - n_chunk + UP_SLOTS, step - n_chunk + UP_SLOTS)
@@ -334,10 +341,8 @@
             pltpu.make_async_copy(wo_hbm.at[:, pl.ds(0, cols)], w_s.at[slot, pl.ds(n_ff, n_ctx), dst], w_sem.at[slot]).wait()
             pltpu.make_async_copy(wd_hbm.at[:, pl.ds(0, cols)], w_s.at[slot, pl.ds(0, n_ff), dst], w_sem.at[slot]).wait()
 
-    for p in range(1, W_SLOTS):
-        w_start(p)
+    w_start(1)
     x_in = pltpu.make_async_copy(x_hbm, x_s, in_sem.at[0])
-    x_in.start()
 
     barrier = pltpu.get_barrier_semaphore()
     for peer in (mate, far):
@@ -368,7 +373,10 @@
         copy1(p).start()
 
     partial(0, w0_ref)
+    w_start(2)
     chip_sum(0)
+    w_start(3)
+    x_in.start()
 
     def compute(p, carry):
         w_wait(p)
@@ -388,6 +396,8 @@
     x_in.wait()
 
     def finish(p, carry):
+        copy1(p).wait_send()
+        copy2(p).wait_send()
         copy2(p).wait_recv()
         xs = x_s[:, pl.ds(col_of(p, 1), cols)].astype(F32)
         out_ref[:, pl.ds(col_of(p, 1), cols)] = (xs + (sum_s[p].astype(F32) + other_s[p].astype(F32))).astype(BF16)
@@ -397,8 +407,6 @@
     lax.fori_loop(0, PIECES, finish, 0)
 
     def drain(p, carry):
-        copy1(p).wait_send()
-        copy2(p).wait_send()
         copy3(p, core).wait_send()
         copy3(p, 1 - core).wait_recv()
         return carry

time: 95.3 us -> 95.1 us (level)
  no operation moved by 1% of the time
where the time goes in v7:
time: 95.1 us; the launch traced here: 95 us
  Pallas kernels  93 us (98%)
  local copies, waits for them, and re-layouts  1.32 us (1%)
    pallas_call x1, Pallas kernels, front(): pl.pallas_call(front_kernel, name='front', in_specs=[SMEM] + [HBM] * 12,...  61.7 us
    pallas_call x1, Pallas kernels, exchange(): pl.pallas_call(exchange_kernel, name='exchange', in_specs=[HBM, VMEM, VME...  31.4 us

profile of v7, /device:TPU:0, one launch (start us, length us, event | category | flops | bytes accessed | tf_op | source)
XLA Modules:
  0.0 95.0 jit_solution(12993604877209803060)
XLA Ops:
  0.6 61.7 %front.1 = (bf16[131072,128]{1,0:T(8,128)(2,1)}, bf16[131072,128]{1,0:T(8,128)(2,1)}, bf16[256,5120]{1,0:T(8,128)(2,1)S(1)}, bf16[5120,256]{1,0:T(8,128)(2,1)S(1)}) custom-call(s32[256]{0:T(256)} %pos_ref.1, bf16[256,4096]{1,0:T(8,128)(2,1)} %x_hbm.3, f32[1,4096]{1,0:T(1,128)} %bitcast.17, f32[1,4096]{1,0:T(1,128)} %bitcast.18, f32[1,4096]{1,0:T(1,128)} %bitcast.19, ...), custom_call_target="tpu_custom_call" | custom-call | flops 22000001024 | bytes 180000000 | tf_op jit(solution)/shard_map/front/pallas_call | solution.py:267
  62.3 31.4 %exchange.1 = bf16[256,4096]{1,0:T(8,128)(2,1)S(1)} custom-call(bf16[256,4096]{1,0:T(8,128)(2,1)} %x_hbm.3, bf16[256,5120]{1,0:T(8,128)(2,1)S(1)} %get-tuple-element.7.lhs_s, bf16[5120,256]{1,0:T(8,128)(2,1)S(1)} %get-tuple-element.8.w0_ref, bf16[4096,4096]{1,0:T(8,128)(2,1)} %wd_hbm.3, bf16[1024,4096]{1,0:T(8,128)(2,1)} %bitcast.15), custom_call_target="tpu_custom_call" | custom-call | flops 11000000512 | bytes 48000000 | tf_op jit(solution)/shard_map/exchange/pallas_call | solution.py:423
  93.7 1.3 %copy.17 = bf16[256,4096]{1,0:T(8,128)(2,1)} copy(bf16[256,4096]{1,0:T(8,128)(2,1)S(1)} %exchange.1) | data formatting | bytes 4194304

commit v8 on v7

--- a/solution.py
+++ b/solution.py
@@ -19,10 +19,10 @@
 
 QKV_CHUNK = 512
 LN_ROWS = 16
-ROW_BLOCK = 8
-SUB_BLOCKS = 2
-KV_SLOTS = 12
-KV_AHEAD = 8
+ROW_BLOCK = 16
+SUB_BLOCKS = 1
+KV_SLOTS = 6
+KV_AHEAD = 4
 UP_SLOTS = 4
 W_PARTS = 4
 
@@ -92,8 +92,7 @@
 
     for c in wq_order[:2]:
         wq_copy(c).start()
-    for i in range(2):
-        start_in(i, i)
+    start_in(0, 0)
 
     freq_in.wait()
 
@@ -112,8 +111,7 @@
         c.wait()
     for c in wq_order[2:4]:
         wq_copy(c).start()
-    for i in range(2, 4):
-        start_in(i, i)
+    start_in(1, 1)
 
     def ln_body(i, carry):
         r = pl.ds(pl.multiple_of(i * LN_ROWS, LN_ROWS), LN_ROWS)
@@ -130,14 +128,16 @@
     lax.fori_loop(0, half_ln, ln_body, 0)
     for c in wq_order[4:]:
         wq_copy(c).start()
-    for i in range(4, 6):
+    free = wq_base // lines_blk
+    for i in range(2, free):
         start_in(i, i)
     lax.fori_loop(half_ln, 2 * half_ln, ln_body, 0)
 
     for step, c in enumerate(wq_order):
         wq_copy(c).wait()
-        if 6 <= step < KV_AHEAD:
-            start_in(step, step)
+        if step == n_chunk - 2:
+            for i in range(free, KV_AHEAD):
+                start_in(i, i)
         if step >= n_chunk - UP_SLOTS:
             up_start(step - n_chunk + UP_SLOTS, step - n_chunk + UP_SLOTS)
         wqf_s[...] = wq_view(c)[...].astype(F32)
@@ -305,6 +305,7 @@
 
 
 PIECES = 16
+GROUPS = ((0, 1), (1, 2), (3, 5), (8, 5), (13, 2), (15, 1))
 W_SLOTS = 4
 MESH = pl.DeviceIdType.MESH
 
@@ -352,8 +353,9 @@
     def copy1(p):
         return pltpu.make_async_remote_copy(send_s.at[p], recv_s.at[p], c1_send.at[p], c1_recv.at[p], device_id={'tp': mate}, device_id_type=MESH)
 
-    def copy2(p):
-        return pltpu.make_async_remote_copy(sum_s.at[p], other_s.at[p], c2_send.at[p], c2_recv.at[p], device_id={'tp': far}, device_id_type=MESH)
+    def copy2(i):
+        pieces = pl.ds(*GROUPS[i])
+        return pltpu.make_async_remote_copy(sum_s.at[pieces], other_s.at[pieces], c2_send.at[i], c2_recv.at[i], device_id={'tp': far}, device_id_type=MESH)
 
     def copy3(p, side):
         view = out_ref.at[:, pl.ds(pl.multiple_of(side * half + p * cols, cols), cols)]
@@ -362,7 +364,10 @@
     def chip_sum(p):
         copy1(p).wait_recv()
         sum_s[p] = (keep_s[p] + recv_s[p].astype(F32)).astype(BF16)
-        copy2(p).start()
+        for i, (a, n) in enumerate(GROUPS):
+            @pl.when(p == a + n - 1)
+            def _():
+                copy2(i).start()
 
     def partial(p, w):
         deep = (n_ff + n_ctx) // 2
@@ -397,14 +402,15 @@
 
     def finish(p, carry):
         copy1(p).wait_send()
-        copy2(p).wait_send()
-        copy2(p).wait_recv()
         xs = x_s[:, pl.ds(col_of(p, 1), cols)].astype(F32)
         out_ref[:, pl.ds(col_of(p, 1), cols)] = (xs + (sum_s[p].astype(F32) + other_s[p].astype(F32))).astype(BF16)
         copy3(p, core).start()
         return carry
 
-    lax.fori_loop(0, PIECES, finish, 0)
+    for i, (a, n) in enumerate(GROUPS):
+        copy2(i).wait_send()
+        copy2(i).wait_recv()
+        lax.fori_loop(a, a + n, finish, 0)
 
     def drain(p, carry):
         copy3(p, core).wait_send()
@@ -435,7 +441,7 @@
             pltpu.VMEM((PIECES, rows, cols), BF16),
             pltpu.VMEM((PIECES, rows, cols), BF16),
             dma((1,)), dma((W_SLOTS,)),
-            dma((PIECES,)), dma((PIECES,)), dma((PIECES,)), dma((PIECES,)), dma((PIECES,)), dma((PIECES,)),
+            dma((PIECES,)), dma((PIECES,)), dma((len(GROUPS),)), dma((len(GROUPS),)), dma((PIECES,)), dma((PIECES,)),
         ],
         compiler_params=pltpu.CompilerParams(vmem_limit_bytes=32 * MIB, collective_id=0, has_side_effects=True),
         cost_estimate=pl.CostEstimate(flops=11 * 10 ** 9, bytes_accessed=48 * 10 ** 6, transcendentals=0),

time: 95.1 us -> 97.7 us (1.027)
  Pallas kernels: 93 us -> 95.6 us
    pallas_call x1, Pallas kernels: 31.4 us -> 34.3 us  [exchange(): pl.pallas_call(exchange_kernel, name='exchange', in_specs=[HBM, VMEM, VME...]
where the time goes in v8:
time: 97.7 us; the launch traced here: 97.5 us
  Pallas kernels  95.6 us (98%)
  local copies, waits for them, and re-layouts  1.32 us (1%)
    pallas_call x1, Pallas kernels, front(): pl.pallas_call(front_kernel, name='front', in_specs=[SMEM] + [HBM] * 12,...  61.2 us
    pallas_call x1, Pallas kernels, exchange(): pl.pallas_call(exchange_kernel, name='exchange', in_specs=[HBM, VMEM, VME...  34.3 us

profile of v8, /device:TPU:0, one launch (start us, length us, event | category | flops | bytes accessed | tf_op | source)
XLA Modules:
  0.0 97.5 jit_solution(3464703783769243086)
XLA Ops:
  0.6 61.2 %front.1 = (bf16[131072,128]{1,0:T(8,128)(2,1)}, bf16[131072,128]{1,0:T(8,128)(2,1)}, bf16[256,5120]{1,0:T(8,128)(2,1)S(1)}, bf16[5120,256]{1,0:T(8,128)(2,1)S(1)}) custom-call(s32[256]{0:T(256)} %pos_ref.1, bf16[256,4096]{1,0:T(8,128)(2,1)} %x_hbm.3, f32[1,4096]{1,0:T(1,128)} %bitcast.17, f32[1,4096]{1,0:T(1,128)} %bitcast.18, f32[1,4096]{1,0:T(1,128)} %bitcast.19, ...), custom_call_target="tpu_custom_call" | custom-call | flops 22000001024 | bytes 180000000 | tf_op jit(solution)/shard_map/front/pallas_call | solution.py:267
  61.9 34.3 %exchange.1 = bf16[256,4096]{1,0:T(8,128)(2,1)S(1)} custom-call(bf16[256,4096]{1,0:T(8,128)(2,1)} %x_hbm.3, bf16[256,5120]{1,0:T(8,128)(2,1)S(1)} %get-tuple-element.7.lhs_s, bf16[5120,256]{1,0:T(8,128)(2,1)S(1)} %get-tuple-element.8.w0_ref, bf16[4096,4096]{1,0:T(8,128)(2,1)} %wd_hbm.3, bf16[1024,4096]{1,0:T(8,128)(2,1)} %bitcast.15), custom_call_target="tpu_custom_call" | custom-call | flops 11000000512 | bytes 48000000 | tf_op jit(solution)/shard_map/exchange/pallas_call | solution.py:429
  96.2 1.3 %copy.17 = bf16[256,4096]{1,0:T(8,128)(2,1)} copy(bf16[256,4096]{1,0:T(8,128)(2,1)S(1)} %exchange.1) | data formatting | bytes 4194304

commit v9 on v8

--- a/solution.py
+++ b/solution.py
@@ -273,7 +273,7 @@
             jax.ShapeDtypeStruct(kc.shape, BF16),
             jax.ShapeDtypeStruct(vc.shape, BF16),
             jax.ShapeDtypeStruct((rows, hid + wo.shape[0]), BF16),
-            jax.ShapeDtypeStruct((hid + wo.shape[0], width // PIECES), BF16),
+            jax.ShapeDtypeStruct((hid + wo.shape[0], 2 * width // PIECES), BF16),
         ],
         scratch_shapes=[
             pltpu.VMEM((rows, width), BF16),
@@ -305,8 +305,8 @@
 
 
 PIECES = 16
-GROUPS = ((0, 1), (1, 2), (3, 5), (8, 5), (13, 2), (15, 1))
-W_SLOTS = 4
+GROUPS = ((0, 1), (1, 1), (2, 2), (4, 2), (6, 2), (8, 2), (10, 2), (12, 2), (14, 1), (15, 1))
+W_SLOTS = 3
 MESH = pl.DeviceIdType.MESH
 
 
@@ -326,21 +326,21 @@
         side = core if part else 1 - core
         return pl.multiple_of(side * half + p * cols, cols)
 
-    def w_start(p):
-        slot = lax.rem(p, W_SLOTS)
+    def w_start(q):
+        slot = lax.rem(q, W_SLOTS)
         for part in range(2):
-            src, dst = pl.ds(col_of(p, part), cols), pl.ds(part * cols, cols)
+            src, dst = pl.ds(col_of(2 * q, part), 2 * cols), pl.ds(2 * part * cols, 2 * cols)
             pltpu.make_async_copy(wo_hbm.at[:, src], w_s.at[slot, pl.ds(n_ff, n_ctx), dst], w_sem.at[slot]).start()
-            for k in range(2):
-                deep = pl.ds(k * (n_ff // 2), n_ff // 2)
+            for k in range(W_PARTS):
+                deep = pl.ds(k * (n_ff // W_PARTS), n_ff // W_PARTS)
                 pltpu.make_async_copy(wd_hbm.at[deep, src], w_s.at[slot, deep, dst], w_sem.at[slot]).start()
 
-    def w_wait(p):
-        slot = lax.rem(p, W_SLOTS)
+    def w_wait(q):
+        slot = lax.rem(q, W_SLOTS)
         for part in range(2):
-            dst = pl.ds(part * cols, cols)
-            pltpu.make_async_copy(wo_hbm.at[:, pl.ds(0, cols)], w_s.at[slot, pl.ds(n_ff, n_ctx), dst], w_sem.at[slot]).wait()
-            pltpu.make_async_copy(wd_hbm.at[:, pl.ds(0, cols)], w_s.at[slot, pl.ds(0, n_ff), dst], w_sem.at[slot]).wait()
+            src, dst = pl.ds(0, 2 * cols), pl.ds(2 * part * cols, 2 * cols)
+            pltpu.make_async_copy(wo_hbm.at[:, src], w_s.at[slot, pl.ds(n_ff, n_ctx), dst], w_sem.at[slot]).wait()
+            pltpu.make_async_copy(wd_hbm.at[:, src], w_s.at[slot, pl.ds(0, n_ff), dst], w_sem.at[slot]).wait()
 
     w_start(1)
     x_in = pltpu.make_async_copy(x_hbm, x_s, in_sem.at[0])
@@ -369,34 +369,36 @@
             def _():
                 copy2(i).start()
 
-    def partial(p, w):
+    def partial(p, w, e):
         deep = (n_ff + n_ctx) // 2
-        s = (jnp.dot(lhs_s[:, :deep], w[:deep, :], preferred_element_type=F32)
-             + jnp.dot(lhs_s[:, deep:], w[deep:, :], preferred_element_type=F32))
+        s = None
+        for k in range(2):
+            rng = slice(k * deep, (k + 1) * deep)
+            rhs = jnp.concatenate([w[rng, (2 * part + e) * cols:(2 * part + e + 1) * cols] for part in range(2)], axis=1)
+            d = jnp.dot(lhs_s[:, rng], rhs, preferred_element_type=F32)
+            s = d if s is None else s + d
         send_s[p] = s[:, :cols].astype(BF16)
         keep_s[p] = s[:, cols:]
         copy1(p).start()
 
-    partial(0, w0_ref)
+    partial(0, w0_ref, 0)
     w_start(2)
+    partial(1, w0_ref, 1)
     chip_sum(0)
-    w_start(3)
     x_in.start()
 
-    def compute(p, carry):
-        w_wait(p)
-
-        @pl.when(p + 3 < PIECES)
+    def compute(q, carry):
+        w_wait(q)
+
+        @pl.when(q + 2 < PIECES // 2)
         def _():
-            w_start(p + 3)
-        partial(p, w_s.at[lax.rem(p, W_SLOTS)])
-
-        @pl.when(p > 1)
-        def _():
-            chip_sum(p - 1)
-        return carry
-
-    lax.fori_loop(1, PIECES, compute, 0)
+            w_start(q + 2)
+        for e in range(2):
+            partial(2 * q + e, w_s.at[lax.rem(q, W_SLOTS)], e)
+            chip_sum(2 * q + e - 1)
+        return carry
+
+    lax.fori_loop(1, PIECES // 2, compute, 0)
     chip_sum(PIECES - 1)
     x_in.wait()
 
@@ -434,7 +436,7 @@
         out_shape=jax.ShapeDtypeStruct((rows, width), BF16),
         scratch_shapes=[
             pltpu.VMEM((rows, width), BF16),
-            pltpu.VMEM((W_SLOTS, n_ff + n_ctx, 2 * cols), BF16),
+            pltpu.VMEM((W_SLOTS, n_ff + n_ctx, 4 * cols), BF16),
             pltpu.VMEM((PIECES, rows, cols), BF16),
             pltpu.VMEM((PIECES, rows, cols), BF16),
             pltpu.VMEM((PIECES, rows, cols), F32),

time: 97.7 us -> 98.5 us (level)
  no operation moved by 1% of the time
where the time goes in v9:
time: 98.5 us; the launch traced here: 98.4 us
  Pallas kernels  96.4 us (98%)
  local copies, waits for them, and re-layouts  1.32 us (1%)
    pallas_call x1, Pallas kernels, front(): pl.pallas_call(front_kernel, name='front', in_specs=[SMEM] + [HBM] * 12,...  61.3 us
    pallas_call x1, Pallas kernels, exchange(): pl.pallas_call(exchange_kernel, name='exchange', in_specs=[HBM, VMEM, VME...  35.2 us

profile of v9, /device:TPU:0, one launch (start us, length us, event | category | flops | bytes accessed | tf_op | source)
XLA Modules:
  0.0 98.4 jit_solution(17088276288141007691)
XLA Ops:
  0.6 61.3 %front.1 = (bf16[131072,128]{1,0:T(8,128)(2,1)}, bf16[131072,128]{1,0:T(8,128)(2,1)}, bf16[256,5120]{1,0:T(8,128)(2,1)S(1)}, bf16[5120,512]{1,0:T(8,128)(2,1)S(1)}) custom-call(s32[256]{0:T(256)} %pos_ref.1, bf16[256,4096]{1,0:T(8,128)(2,1)} %x_hbm.3, f32[1,4096]{1,0:T(1,128)} %bitcast.17, f32[1,4096]{1,0:T(1,128)} %bitcast.18, f32[1,4096]{1,0:T(1,128)} %bitcast.19, ...), custom_call_target="tpu_custom_call" | custom-call | flops 22000001024 | bytes 180000000 | tf_op jit(solution)/shard_map/front/pallas_call | solution.py:267
  61.9 35.2 %exchange.1 = bf16[256,4096]{1,0:T(8,128)(2,1)S(1)} custom-call(bf16[256,4096]{1,0:T(8,128)(2,1)} %x_hbm.3, bf16[256,5120]{1,0:T(8,128)(2,1)S(1)} %get-tuple-element.7.lhs_s, bf16[5120,512]{1,0:T(8,128)(2,1)S(1)} %get-tuple-element.8.w0_ref, bf16[4096,4096]{1,0:T(8,128)(2,1)} %wd_hbm.3, bf16[1024,4096]{1,0:T(8,128)(2,1)} %bitcast.15), custom_call_target="tpu_custom_call" | custom-call | flops 11000000512 | bytes 48000000 | tf_op jit(solution)/shard_map/exchange/pallas_call | solution.py:431
  97.1 1.3 %copy.17 = bf16[256,4096]{1,0:T(8,128)(2,1)} copy(bf16[256,4096]{1,0:T(8,128)(2,1)S(1)} %exchange.1) | data formatting | bytes 4194304

commit v10 on v8

--- a/solution.py
+++ b/solution.py
@@ -305,8 +305,7 @@
 
 
 PIECES = 16
-GROUPS = ((0, 1), (1, 2), (3, 5), (8, 5), (13, 2), (15, 1))
-W_SLOTS = 4
+W_SLOTS = 3
 MESH = pl.DeviceIdType.MESH
 
 
@@ -353,9 +352,8 @@
     def copy1(p):
         return pltpu.make_async_remote_copy(send_s.at[p], recv_s.at[p], c1_send.at[p], c1_recv.at[p], device_id={'tp': mate}, device_id_type=MESH)
 
-    def copy2(i):
-        pieces = pl.ds(*GROUPS[i])
-        return pltpu.make_async_remote_copy(sum_s.at[pieces], other_s.at[pieces], c2_send.at[i], c2_recv.at[i], device_id={'tp': far}, device_id_type=MESH)
+    def copy2(p):
+        return pltpu.make_async_remote_copy(sum_s.at[p], other_s.at[p], c2_send.at[p], c2_recv.at[p], device_id={'tp': far}, device_id_type=MESH)
 
     def copy3(p, side):
         view = out_ref.at[:, pl.ds(pl.multiple_of(side * half + p * cols, cols), cols)]
@@ -364,10 +362,7 @@
     def chip_sum(p):
         copy1(p).wait_recv()
         sum_s[p] = (keep_s[p] + recv_s[p].astype(F32)).astype(BF16)
-        for i, (a, n) in enumerate(GROUPS):
-            @pl.when(p == a + n - 1)
-            def _():
-                copy2(i).start()
+        copy2(p).start()
 
     def partial(p, w):
         deep = (n_ff + n_ctx) // 2
@@ -380,37 +375,40 @@
     partial(0, w0_ref)
     w_start(2)
     chip_sum(0)
-    w_start(3)
     x_in.start()
 
     def compute(p, carry):
         w_wait(p)
 
-        @pl.when(p + 3 < PIECES)
+        @pl.when(p + 2 < PIECES)
         def _():
-            w_start(p + 3)
+            w_start(p + 2)
         partial(p, w_s.at[lax.rem(p, W_SLOTS)])
 
-        @pl.when(p > 1)
+        @pl.when(p == 2)
         def _():
-            chip_sum(p - 1)
+            chip_sum(1)
+
+        @pl.when(p > 3)
+        def _():
+            chip_sum(p - 2)
         return carry
 
     lax.fori_loop(1, PIECES, compute, 0)
+    chip_sum(PIECES - 2)
     chip_sum(PIECES - 1)
     x_in.wait()
 
     def finish(p, carry):
         copy1(p).wait_send()
+        copy2(p).wait_send()
+        copy2(p).wait_recv()
         xs = x_s[:, pl.ds(col_of(p, 1), cols)].astype(F32)
         out_ref[:, pl.ds(col_of(p, 1), cols)] = (xs + (sum_s[p].astype(F32) + other_s[p].astype(F32))).astype(BF16)
         copy3(p, core).start()
         return carry
 
-    for i, (a, n) in enumerate(GROUPS):
-        copy2(i).wait_send()
-        copy2(i).wait_recv()
-        lax.fori_loop(a, a + n, finish, 0)
+    lax.fori_loop(0, PIECES, finish, 0)
 
     def drain(p, carry):
         copy3(p, core).wait_send()
@@ -441,7 +439,7 @@
             pltpu.VMEM((PIECES, rows, cols), BF16),
             pltpu.VMEM((PIECES, rows, cols), BF16),
             dma((1,)), dma((W_SLOTS,)),
-            dma((PIECES,)), dma((PIECES,)), dma((len(GROUPS),)), dma((len(GROUPS),)), dma((PIECES,)), dma((PIECES,)),
+            dma((PIECES,)), dma((PIECES,)), dma((PIECES,)), dma((PIECES,)), dma((PIECES,)), dma((PIECES,)),
         ],
         compiler_params=pltpu.CompilerParams(vmem_limit_bytes=32 * MIB, collective_id=0, has_side_effects=True),
         cost_estimate=pl.CostEstimate(flops=11 * 10 ** 9, bytes_accessed=48 * 10 ** 6, transcendentals=0),

time: 97.7 us -> 95.5 us (0.977)
  Pallas kernels: 95.6 us -> 93.4 us
    pallas_call x1, Pallas kernels: 34.3 us -> 32.2 us  [exchange(): pl.pallas_call(exchange_kernel, name='exchange', in_specs=[HBM, VMEM, VME...]
where the time goes in v10:
time: 95.5 us; the launch traced here: 95.4 us
  Pallas kernels  93.4 us (98%)
  local copies, waits for them, and re-layouts  1.32 us (1%)
    pallas_call x1, Pallas kernels, front(): pl.pallas_call(front_kernel, name='front', in_specs=[SMEM] + [HBM] * 12,...  61.2 us
    pallas_call x1, Pallas kernels, exchange(): pl.pallas_call(exchange_kernel, name='exchange', in_specs=[HBM, VMEM, VME...  32.2 us

profile of v10, /device:TPU:0, one launch (start us, length us, event | category | flops | bytes accessed | tf_op | source)
XLA Modules:
  0.0 95.4 jit_solution(18030763053028795978)
XLA Ops:
  0.6 61.2 %front.1 = (bf16[131072,128]{1,0:T(8,128)(2,1)}, bf16[131072,128]{1,0:T(8,128)(2,1)}, bf16[256,5120]{1,0:T(8,128)(2,1)S(1)}, bf16[5120,256]{1,0:T(8,128)(2,1)S(1)}) custom-call(s32[256]{0:T(256)} %pos_ref.1, bf16[256,4096]{1,0:T(8,128)(2,1)} %x_hbm.3, f32[1,4096]{1,0:T(1,128)} %bitcast.17, f32[1,4096]{1,0:T(1,128)} %bitcast.18, f32[1,4096]{1,0:T(1,128)} %bitcast.19, ...), custom_call_target="tpu_custom_call" | custom-call | flops 22000001024 | bytes 180000000 | tf_op jit(solution)/shard_map/front/pallas_call | solution.py:267
  61.9 32.2 %exchange.1 = bf16[256,4096]{1,0:T(8,128)(2,1)S(1)} custom-call(bf16[256,4096]{1,0:T(8,128)(2,1)} %x_hbm.3, bf16[256,5120]{1,0:T(8,128)(2,1)S(1)} %get-tuple-element.7.lhs_s, bf16[5120,256]{1,0:T(8,128)(2,1)S(1)} %get-tuple-element.8.w0_ref, bf16[4096,4096]{1,0:T(8,128)(2,1)} %wd_hbm.3, bf16[1024,4096]{1,0:T(8,128)(2,1)} %bitcast.15), custom_call_target="tpu_custom_call" | custom-call | flops 11000000512 | bytes 48000000 | tf_op jit(solution)/shard_map/exchange/pallas_call | solution.py:427
  94.1 1.3 %copy.17 = bf16[256,4096]{1,0:T(8,128)(2,1)} copy(bf16[256,4096]{1,0:T(8,128)(2,1)S(1)} %exchange.1) | data formatting | bytes 4194304

commit v11 on v10

--- a/solution.py
+++ b/solution.py
@@ -20,10 +20,10 @@
 QKV_CHUNK = 512
 LN_ROWS = 16
 ROW_BLOCK = 16
-SUB_BLOCKS = 1
-KV_SLOTS = 6
-KV_AHEAD = 4
-UP_SLOTS = 4
+KV_SLOTS = 7
+KV_AHEAD = 5
+UP_SLOTS = 3
+UP_EARLY = 3
 W_PARTS = 4
 
 
@@ -209,46 +209,55 @@
         w0_in.append(pltpu.make_async_copy(wd_hbm.at[:, src], w0_ref.at[pl.ds(0, n_ff), dst], w0_sem.at[0]))
         w0_in.append(pltpu.make_async_copy(wo_hbm.at[:, src], w0_ref.at[pl.ds(n_ff, wo_hbm.shape[0]), dst], w0_sem.at[0]))
 
-    def body(i, carry):
-        for s in range(SUB_BLOCKS):
-            nxt = i * SUB_BLOCKS + s + KV_AHEAD
-
-            @pl.when(nxt < n_blk)
-            def _():
-                nslot = lax.rem(nxt, KV_SLOTS)
-
-                @pl.when(nxt >= KV_SLOTS)
-                def _():
-                    wait_out(nslot)
-                start_in(nxt, nslot)
-
-        @pl.when((i >= 1) & (i - 1 + UP_SLOTS < n_up))
-        def _():
-            up_start(i - 1 + UP_SLOTS, lax.rem(i - 1, UP_SLOTS))
-
-        uslot = lax.rem(i, UP_SLOTS)
-        up_wait(uslot)
-        for s in range(SUB_BLOCKS):
-            wait_in(lax.rem(i * SUB_BLOCKS + s, KV_SLOTS))
+    def up_block(b):
+        uslot = lax.rem(b, UP_SLOTS)
         deep = width // 2
         pre = (jnp.dot(mlp_s[:, :deep], up_s[uslot, :deep, :], preferred_element_type=F32)
                + jnp.dot(mlp_s[:, deep:], up_s[uslot, deep:, :], preferred_element_type=F32))
         act = 0.5 * pre * (1.0 + lax.erf(pre * (0.5 ** 0.5)))
-        lhs_ref[:, pl.ds(pl.multiple_of(i * up_cols, up_cols), up_cols)] = act.astype(BF16)
-        for s in range(SUB_BLOCKS):
-            blk = i * SUB_BLOCKS + s
-            attend_block(blk, lax.rem(blk, KV_SLOTS))
-        for s in range(SUB_BLOCKS):
-            blk = i * SUB_BLOCKS + s
-            start_out(blk, lax.rem(blk, KV_SLOTS))
-
-        @pl.when(i == n_up - 4)
+        lhs_ref[:, pl.ds(pl.multiple_of(b * up_cols, up_cols), up_cols)] = act.astype(BF16)
+
+    def body(i, carry, with_up):
+        nxt = i + KV_AHEAD
+
+        @pl.when(nxt < n_blk)
+        def _():
+            nslot = lax.rem(nxt, KV_SLOTS)
+
+            @pl.when(nxt >= KV_SLOTS)
+            def _():
+                wait_out(nslot)
+            start_in(nxt, nslot)
+
+        slot = lax.rem(i, KV_SLOTS)
+        if with_up:
+            b = i + UP_EARLY
+
+            @pl.when(b - 1 + UP_SLOTS < n_up)
+            def _():
+                up_start(b - 1 + UP_SLOTS, lax.rem(b - 1, UP_SLOTS))
+
+            up_wait(lax.rem(b, UP_SLOTS))
+            wait_in(slot)
+            up_block(b)
+        else:
+            wait_in(slot)
+        attend_block(i, slot)
+        start_out(i, slot)
+
+        @pl.when(i == n_blk - 5)
         def _():
             for c in w0_in:
                 c.start(priority=1)
         return carry
 
-    lax.fori_loop(0, n_up, body, 0)
+    for b in range(UP_EARLY):
+        up_wait(b % UP_SLOTS)
+        up_block(b)
+        if b:
+            up_start(b - 1 + UP_SLOTS, (b - 1) % UP_SLOTS)
+    lax.fori_loop(0, n_blk - UP_EARLY, lambda i, c: body(i, c, True), 0)
+    lax.fori_loop(n_blk - UP_EARLY, n_blk, lambda i, c: body(i, c, False), 0)
     for h in range(ctx_s.shape[0] // rows):
         lhs_ref[:, n_ff + h * 128:n_ff + (h + 1) * 128] = ctx_s[h * rows:(h + 1) * rows, :].astype(BF16)
     for c in w0_in:
@@ -262,7 +271,7 @@
     hid = wu.shape[1]
     lines = wq.shape[0] // width
     n_head = (lines // 2 - 2) * 2
-    up_cols = hid // (rows // (ROW_BLOCK * SUB_BLOCKS))
+    up_cols = hid // (rows // ROW_BLOCK)
     lines_blk = kc.shape[0] // rows * ROW_BLOCK
     return pl.pallas_call(
         front_kernel,
@@ -299,13 +308,13 @@
             pltpu.SemaphoreType.DMA((KV_SLOTS,)),
             pltpu.SemaphoreType.DMA((1,)),
         ],
-        compiler_params=pltpu.CompilerParams(vmem_limit_bytes=44 * MIB),
+        compiler_params=pltpu.CompilerParams(vmem_limit_bytes=47 * MIB),
         cost_estimate=pl.CostEstimate(flops=22 * 10 ** 9, bytes_accessed=180 * 10 ** 6, transcendentals=0),
     )(pos, x, ga, ba, gm, bm, freq, wq, wu, wd, wo, kc, vc)
 
 
 PIECES = 16
-W_SLOTS = 3
+W_SLOTS = 4
 MESH = pl.DeviceIdType.MESH
 
 
@@ -375,27 +384,23 @@
     partial(0, w0_ref)
     w_start(2)
     chip_sum(0)
+    w_start(3)
     x_in.start()
 
     def compute(p, carry):
         w_wait(p)
 
-        @pl.when(p + 2 < PIECES)
+        @pl.when(p + 3 < PIECES)
         def _():
-            w_start(p + 2)
+            w_start(p + 3)
         partial(p, w_s.at[lax.rem(p, W_SLOTS)])
 
-        @pl.when(p == 2)
+        @pl.when(p > 1)
         def _():
-            chip_sum(1)
-
-        @pl.when(p > 3)
-        def _():
-            chip_sum(p - 2)
+            chip_sum(p - 1)
         return carry
 
     lax.fori_loop(1, PIECES, compute, 0)
-    chip_sum(PIECES - 2)
     chip_sum(PIECES - 1)
     x_in.wait()
 

time: 95.5 us -> 96.6 us (1.012)
  Pallas kernels: 93.4 us -> 94.5 us
    pallas_call x1, Pallas kernels: 61.2 us -> 63.1 us  [front(): pl.pallas_call(front_kernel, name='front', in_specs=[SMEM] + [HBM] * 12,...]
where the time goes in v11:
time: 96.6 us; the launch traced here: 96.5 us
  Pallas kernels  94.5 us (98%)
  local copies, waits for them, and re-layouts  1.32 us (1%)
    pallas_call x1, Pallas kernels, front(): pl.pallas_call(front_kernel, name='front', in_specs=[SMEM] + [HBM] * 12,...  63.1 us
    pallas_call x1, Pallas kernels, exchange(): pl.pallas_call(exchange_kernel, name='exchange', in_specs=[HBM, VMEM, VME...  31.4 us

profile of v11, /device:TPU:0, one launch (start us, length us, event | category | flops | bytes accessed | tf_op | source)
XLA Modules:
  0.0 96.5 jit_solution(12159176714399264826)
XLA Ops:
  0.6 63.1 %front.1 = (bf16[131072,128]{1,0:T(8,128)(2,1)}, bf16[131072,128]{1,0:T(8,128)(2,1)}, bf16[256,5120]{1,0:T(8,128)(2,1)S(1)}, bf16[5120,256]{1,0:T(8,128)(2,1)S(1)}) custom-call(s32[256]{0:T(256)} %pos_ref.1, bf16[256,4096]{1,0:T(8,128)(2,1)} %x_hbm.3, f32[1,4096]{1,0:T(1,128)} %bitcast.17, f32[1,4096]{1,0:T(1,128)} %bitcast.18, f32[1,4096]{1,0:T(1,128)} %bitcast.19, ...), custom_call_target="tpu_custom_call" | custom-call | flops 22000001024 | bytes 180000000 | tf_op jit(solution)/shard_map/front/pallas_call | solution.py:276
  63.8 31.4 %exchange.1 = bf16[256,4096]{1,0:T(8,128)(2,1)S(1)} custom-call(bf16[256,4096]{1,0:T(8,128)(2,1)} %x_hbm.3, bf16[256,5120]{1,0:T(8,128)(2,1)S(1)} %get-tuple-element.7.lhs_s, bf16[5120,256]{1,0:T(8,128)(2,1)S(1)} %get-tuple-element.8.w0_ref, bf16[4096,4096]{1,0:T(8,128)(2,1)} %wd_hbm.3, bf16[1024,4096]{1,0:T(8,128)(2,1)} %bitcast.15), custom_call_target="tpu_custom_call" | custom-call | flops 11000000512 | bytes 48000000 | tf_op jit(solution)/shard_map/exchange/pallas_call | solution.py:432
  95.2 1.3 %copy.17 = bf16[256,4096]{1,0:T(8,128)(2,1)} copy(bf16[256,4096]{1,0:T(8,128)(2,1)S(1)} %exchange.1) | data formatting | bytes 4194304

commit v12 on v11

--- a/solution.py
+++ b/solution.py
@@ -23,7 +23,6 @@
 KV_SLOTS = 7
 KV_AHEAD = 5
 UP_SLOTS = 3
-UP_EARLY = 3
 W_PARTS = 4
 
 
@@ -217,7 +216,7 @@
         act = 0.5 * pre * (1.0 + lax.erf(pre * (0.5 ** 0.5)))
         lhs_ref[:, pl.ds(pl.multiple_of(b * up_cols, up_cols), up_cols)] = act.astype(BF16)
 
-    def body(i, carry, with_up):
+    def body(i, carry):
         nxt = i + KV_AHEAD
 
         @pl.when(nxt < n_blk)
@@ -230,18 +229,14 @@
             start_in(nxt, nslot)
 
         slot = lax.rem(i, KV_SLOTS)
-        if with_up:
-            b = i + UP_EARLY
-
-            @pl.when(b - 1 + UP_SLOTS < n_up)
-            def _():
-                up_start(b - 1 + UP_SLOTS, lax.rem(b - 1, UP_SLOTS))
-
-            up_wait(lax.rem(b, UP_SLOTS))
-            wait_in(slot)
-            up_block(b)
-        else:
-            wait_in(slot)
+
+        @pl.when((i >= 1) & (i - 1 + UP_SLOTS < n_up))
+        def _():
+            up_start(i - 1 + UP_SLOTS, lax.rem(i - 1, UP_SLOTS))
+
+        up_wait(lax.rem(i, UP_SLOTS))
+        wait_in(slot)
+        up_block(i)
         attend_block(i, slot)
         start_out(i, slot)
 
@@ -251,13 +246,7 @@
                 c.start(priority=1)
         return carry
 
-    for b in range(UP_EARLY):
-        up_wait(b % UP_SLOTS)
-        up_block(b)
-        if b:
-            up_start(b - 1 + UP_SLOTS, (b - 1) % UP_SLOTS)
-    lax.fori_loop(0, n_blk - UP_EARLY, lambda i, c: body(i, c, True), 0)
-    lax.fori_loop(n_blk - UP_EARLY, n_blk, lambda i, c: body(i, c, False), 0)
+    lax.fori_loop(0, n_blk, body, 0)
     for h in range(ctx_s.shape[0] // rows):
         lhs_ref[:, n_ff + h * 128:n_ff + (h + 1) * 128] = ctx_s[h * rows:(h + 1) * rows, :].astype(BF16)
     for c in w0_in:

time: 96.6 us -> 95.4 us (0.988)
  Pallas kernels: 94.5 us -> 93.4 us
    pallas_call x1, Pallas kernels: 63.1 us -> 61.7 us  [front(): pl.pallas_call(front_kernel, name='front', in_specs=[SMEM] + [HBM] * 12,...]
where the time goes in v12:
time: 95.4 us; the launch traced here: 95.3 us
  Pallas kernels  93.4 us (98%)
  local copies, waits for them, and re-layouts  1.32 us (1%)
    pallas_call x1, Pallas kernels, front(): pl.pallas_call(front_kernel, name='front', in_specs=[SMEM] + [HBM] * 12,...  61.7 us
    pallas_call x1, Pallas kernels, exchange(): pl.pallas_call(exchange_kernel, name='exchange', in_specs=[HBM, VMEM, VME...  31.6 us

profile of v12, /device:TPU:0, one launch (start us, length us, event | category | flops | bytes accessed | tf_op | source)
XLA Modules:
  0.0 95.3 jit_solution(5806867340986046312)
XLA Ops:
  0.6 61.7 %front.1 = (bf16[131072,128]{1,0:T(8,128)(2,1)}, bf16[131072,128]{1,0:T(8,128)(2,1)}, bf16[256,5120]{1,0:T(8,128)(2,1)S(1)}, bf16[5120,256]{1,0:T(8,128)(2,1)S(1)}) custom-call(s32[256]{0:T(256)} %pos_ref.1, bf16[256,4096]{1,0:T(8,128)(2,1)} %x_hbm.3, f32[1,4096]{1,0:T(1,128)} %bitcast.17, f32[1,4096]{1,0:T(1,128)} %bitcast.18, f32[1,4096]{1,0:T(1,128)} %bitcast.19, ...), custom_call_target="tpu_custom_call" | custom-call | flops 22000001024 | bytes 180000000 | tf_op jit(solution)/shard_map/front/pallas_call | solution.py:265
  62.4 31.6 %exchange.1 = bf16[256,4096]{1,0:T(8,128)(2,1)S(1)} custom-call(bf16[256,4096]{1,0:T(8,128)(2,1)} %x_hbm.3, bf16[256,5120]{1,0:T(8,128)(2,1)S(1)} %get-tuple-element.7.lhs_s, bf16[5120,256]{1,0:T(8,128)(2,1)S(1)} %get-tuple-element.8.w0_ref, bf16[4096,4096]{1,0:T(8,128)(2,1)} %wd_hbm.3, bf16[1024,4096]{1,0:T(8,128)(2,1)} %bitcast.15), custom_call_target="tpu_custom_call" | custom-call | flops 11000000512 | bytes 48000000 | tf_op jit(solution)/shard_map/exchange/pallas_call | solution.py:421
  94.0 1.3 %copy.17 = bf16[256,4096]{1,0:T(8,128)(2,1)} copy(bf16[256,4096]{1,0:T(8,128)(2,1)S(1)} %exchange.1) | data formatting | bytes 4194304

commit v13 on v12

--- a/solution.py
+++ b/solution.py
@@ -20,9 +20,9 @@
 QKV_CHUNK = 512
 LN_ROWS = 16
 ROW_BLOCK = 16
-KV_SLOTS = 7
-KV_AHEAD = 5
-UP_SLOTS = 3
+KV_SLOTS = 6
+KV_AHEAD = 4
+UP_SLOTS = 4
 W_PARTS = 4
 
 
@@ -297,7 +297,7 @@
             pltpu.SemaphoreType.DMA((KV_SLOTS,)),
             pltpu.SemaphoreType.DMA((1,)),
         ],
-        compiler_params=pltpu.CompilerParams(vmem_limit_bytes=47 * MIB),
+        compiler_params=pltpu.CompilerParams(vmem_limit_bytes=44 * MIB),
         cost_estimate=pl.CostEstimate(flops=22 * 10 ** 9, bytes_accessed=180 * 10 ** 6, transcendentals=0),
     )(pos, x, ga, ba, gm, bm, freq, wq, wu, wd, wo, kc, vc)
 

time: 95.4 us -> 94.7 us (level)
  no operation moved by 1% of the time
where the time goes in v13:
time: 94.7 us; the launch traced here: 94.6 us
  Pallas kernels  92.6 us (98%)
  local copies, waits for them, and re-layouts  1.32 us (1%)
    pallas_call x1, Pallas kernels, front(): pl.pallas_call(front_kernel, name='front', in_specs=[SMEM] + [HBM] * 12,...  61.2 us
    pallas_call x1, Pallas kernels, exchange(): pl.pallas_call(exchange_kernel, name='exchange', in_specs=[HBM, VMEM, VME...  31.4 us

profile of v13, /device:TPU:0, one launch (start us, length us, event | category | flops | bytes accessed | tf_op | source)
XLA Modules:
  0.0 94.6 jit_solution(6539207188648948061)
XLA Ops:
  0.6 61.2 %front.1 = (bf16[131072,128]{1,0:T(8,128)(2,1)}, bf16[131072,128]{1,0:T(8,128)(2,1)}, bf16[256,5120]{1,0:T(8,128)(2,1)S(1)}, bf16[5120,256]{1,0:T(8,128)(2,1)S(1)}) custom-call(s32[256]{0:T(256)} %pos_ref.1, bf16[256,4096]{1,0:T(8,128)(2,1)} %x_hbm.3, f32[1,4096]{1,0:T(1,128)} %bitcast.17, f32[1,4096]{1,0:T(1,128)} %bitcast.18, f32[1,4096]{1,0:T(1,128)} %bitcast.19, ...), custom_call_target="tpu_custom_call" | custom-call | flops 22000001024 | bytes 180000000 | tf_op jit(solution)/shard_map/front/pallas_call | solution.py:265
  61.9 31.4 %exchange.1 = bf16[256,4096]{1,0:T(8,128)(2,1)S(1)} custom-call(bf16[256,4096]{1,0:T(8,128)(2,1)} %x_hbm.3, bf16[256,5120]{1,0:T(8,128)(2,1)S(1)} %get-tuple-element.7.lhs_s, bf16[5120,256]{1,0:T(8,128)(2,1)S(1)} %get-tuple-element.8.w0_ref, bf16[4096,4096]{1,0:T(8,128)(2,1)} %wd_hbm.3, bf16[1024,4096]{1,0:T(8,128)(2,1)} %bitcast.15), custom_call_target="tpu_custom_call" | custom-call | flops 11000000512 | bytes 48000000 | tf_op jit(solution)/shard_map/exchange/pallas_call | solution.py:421
  93.3 1.3 %copy.17 = bf16[256,4096]{1,0:T(8,128)(2,1)} copy(bf16[256,4096]{1,0:T(8,128)(2,1)S(1)} %exchange.1) | data formatting | bytes 4194304

commit v14 on v13

--- a/solution.py
+++ b/solution.py
@@ -22,7 +22,7 @@
 ROW_BLOCK = 16
 KV_SLOTS = 6
 KV_AHEAD = 4
-UP_SLOTS = 4
+UP_SLOTS = 5
 W_PARTS = 4
 
 
@@ -297,7 +297,7 @@
             pltpu.SemaphoreType.DMA((KV_SLOTS,)),
             pltpu.SemaphoreType.DMA((1,)),
         ],
-        compiler_params=pltpu.CompilerParams(vmem_limit_bytes=44 * MIB),
+        compiler_params=pltpu.CompilerParams(vmem_limit_bytes=46 * MIB),
         cost_estimate=pl.CostEstimate(flops=22 * 10 ** 9, bytes_accessed=180 * 10 ** 6, transcendentals=0),
     )(pos, x, ga, ba, gm, bm, freq, wq, wu, wd, wo, kc, vc)
 

time: 94.7 us -> 94 us (level)
  no operation moved by 1% of the time
where the time goes in v14:
time: 94 us; the launch traced here: 93.9 us
  Pallas kernels  92 us (98%)
  local copies, waits for them, and re-layouts  1.32 us (1%)
    pallas_call x1, Pallas kernels, front(): pl.pallas_call(front_kernel, name='front', in_specs=[SMEM] + [HBM] * 12,...  60.6 us
    pallas_call x1, Pallas kernels, exchange(): pl.pallas_call(exchange_kernel, name='exchange', in_specs=[HBM, VMEM, VME...  31.4 us

profile of v14, /device:TPU:0, one launch (start us, length us, event | category | flops | bytes accessed | tf_op | source)
XLA Modules:
  0.0 93.9 jit_solution(8818368891812690352)
XLA Ops:
  0.6 60.6 %front.1 = (bf16[131072,128]{1,0:T(8,128)(2,1)}, bf16[131072,128]{1,0:T(8,128)(2,1)}, bf16[256,5120]{1,0:T(8,128)(2,1)S(1)}, bf16[5120,256]{1,0:T(8,128)(2,1)S(1)}) custom-call(s32[256]{0:T(256)} %pos_ref.1, bf16[256,4096]{1,0:T(8,128)(2,1)} %x_hbm.3, f32[1,4096]{1,0:T(1,128)} %bitcast.17, f32[1,4096]{1,0:T(1,128)} %bitcast.18, f32[1,4096]{1,0:T(1,128)} %bitcast.19, ...), custom_call_target="tpu_custom_call" | custom-call | flops 22000001024 | bytes 180000000 | tf_op jit(solution)/shard_map/front/pallas_call | solution.py:265
  61.2 31.4 %exchange.1 = bf16[256,4096]{1,0:T(8,128)(2,1)S(1)} custom-call(bf16[256,4096]{1,0:T(8,128)(2,1)} %x_hbm.3, bf16[256,5120]{1,0:T(8,128)(2,1)S(1)} %get-tuple-element.7.lhs_s, bf16[5120,256]{1,0:T(8,128)(2,1)S(1)} %get-tuple-element.8.w0_ref, bf16[4096,4096]{1,0:T(8,128)(2,1)} %wd_hbm.3, bf16[1024,4096]{1,0:T(8,128)(2,1)} %bitcast.15), custom_call_target="tpu_custom_call" | custom-call | flops 11000000512 | bytes 48000000 | tf_op jit(solution)/shard_map/exchange/pallas_call | solution.py:421
  92.6 1.3 %copy.17 = bf16[256,4096]{1,0:T(8,128)(2,1)} copy(bf16[256,4096]{1,0:T(8,128)(2,1)S(1)} %exchange.1) | data formatting | bytes 4194304
